TPU v7x, 8 devices: a whole 2x2x1 slice. The times are simulated.
8 devices in a mesh: dp: 1 (over z), ep: 2 (over y), tp: 4 (over x, core).
Axes of the slice: x: 2, y: 2, z: 1, core: 2. Of those that a mesh axis runs over, the one named last changes fastest.
Arguments:
- tokens: bfloat16 [8192, 768], P(('dp', 'ep', 'tp'))
- expert_ids: int32 [8192, 4], P(('dp', 'ep', 'tp'))
- gates: float32 [8192, 4], P(('dp', 'ep', 'tp'))
- w_gate: bfloat16 [16, 768, 10752], P('ep', None, 'tp')
- w_up: bfloat16 [16, 768, 10752], P('ep', None, 'tp')
- w_down: bfloat16 [16, 10752, 768], P('ep', 'tp')
Outputs:
- output: bfloat16 [8192, 768], P(('dp', 'ep', 'tp'))
All inputs are finite; a program needn't handle non-finite values.
Results may differ from a plain program's by a relative error of at most 0.00998244.
Values are sent between devices in bfloat16 or wider.
A program may use at most 1 GiB of HBM per device.

v0:
```python
import functools
import jax
import jax.numpy as jnp
from jax import lax
from jax.experimental import pallas as pl
from jax.experimental.pallas import tpu as pltpu

from jax.sharding import PartitionSpec as P


def add_pair(a, b):
    return (a.astype(jnp.float32) + b.astype(jnp.float32)).astype(jnp.bfloat16)


CHUNK = 512
BLOCK = 256
PARTS = 3
WINDOW = 128


def chunks_of(width, step):
    return [(lo, min(step, width - lo)) for lo in range(0, width, step)]


def phase_kernel(cap, small, first, experts, pieces, adds, waits, route_ref, *refs):
    tok_hbm, refs = refs[:pieces], refs[pieces:]
    wg_hbm, wu_hbm, wd_hbm = refs[:3]
    add_hbm = refs[3:3 + adds]
    refs = refs[3 + adds + waits:]
    sources, lines, toks = route_ref.shape
    out_hbm = refs[:sources]
    (wg_buf, wu_buf, wd_buf, tok_ref, rows_ref, pick_ref, yblk_ref, yblk2_ref, acc_ref, slot_lane, gate_lane, slot_sub, row_gate, h_ref,
     base_ref, sems, tok_sems, out_sem, *sum_refs) = refs[sources:]
    top_k = lines // 2
    ff = wg_hbm.shape[2]
    blocks = toks // BLOCK
    stride = cap + WINDOW

    def weight_copies(e, buf):
        copies = []
        for i, (src, dst) in enumerate(((wg_hbm, wg_buf), (wu_hbm, wu_buf), (wd_hbm, wd_buf))):
            rows = src.shape[1] // PARTS
            for p in range(PARTS):
                part = pl.ds(p * rows, rows)
                copies.append(pltpu.make_async_copy(src.at[first + e, part, :], dst.at[buf, part, :], sems.at[buf, i * PARTS + p]))
        return copies

    size = sources * toks // pieces
    tok_copies = [
        pltpu.make_async_copy(tok_hbm[p], tok_ref.at[p * size // toks, pl.ds(p * size % toks, size), :], tok_sems.at[p])
        for p in range(pieces)
    ]
    for copy in tok_copies:
        copy.start()

    tri = (lax.broadcasted_iota(jnp.int32, (128, 128), 0) < lax.broadcasted_iota(jnp.int32, (128, 128), 1)).astype(jnp.bfloat16)
    expert_row = (lax.broadcasted_iota(jnp.int32, (experts, toks), 0) + first).astype(jnp.float32)

    def number(s, _):
        hit = jnp.zeros((experts, toks), jnp.float32)
        gate = jnp.zeros((experts, toks), jnp.float32)
        for j in range(top_k):
            same = route_ref[s, j:j + 1, :] == expert_row
            hit = jnp.where(same, 1.0, hit)
            gate = jnp.where(same, route_ref[s, top_k + j:top_k + j + 1, :], gate)
        lanes = [hit[:, lo:lo + 128] for lo in range(0, toks, 128)]
        inner = jnp.dot(jnp.concatenate(lanes, axis=0).astype(jnp.bfloat16), tri, preferred_element_type=jnp.float32)
        base = jnp.zeros((experts, 1), jnp.float32)
        parts = []
        for i in range(len(lanes)):
            if i * 128 % BLOCK == 0:
                for e in range(experts):
                    base_ref[s, i * 128 // BLOCK, e] = base[e, 0].astype(jnp.int32)
            part = inner[i * experts:(i + 1) * experts, :]
            parts.append(part + base)
            base = base + part[:, 127:128] + lanes[i][:, 127:128]
        for e in range(experts):
            base_ref[s, blocks, e] = base[e, 0].astype(jnp.int32)
        slot = jnp.concatenate(parts, axis=1)
        slot = jnp.where((hit > 0) & (slot < cap), slot, -1.0)
        slot_lane[s] = slot
        gate_lane[s] = gate
        slot_sub[s] = jnp.transpose(slot)
        return 0

    lax.fori_loop(0, sources, number, 0)
    rows_ref[...] = jnp.zeros_like(rows_ref)
    row_gate[...] = jnp.zeros_like(row_gate)
    for copy in tok_copies:
        copy.wait()
    for copy in weight_copies(0, 0):
        copy.start()
    if adds:
        add_ref, sum_ref, add_sem = sum_refs
        add_copies = [pltpu.make_async_copy(add_hbm[i], add_ref.at[i], add_sem.at[i]) for i in range(adds)]
        for copy in add_copies:
            copy.start()

    def bounds(s, b, e):
        begin = jnp.minimum(base_ref[s, b, e], cap)
        end = jnp.minimum(base_ref[s, b + 1, e], cap)
        return begin, end, (begin // 16) * 16

    def extra_windows(s, b):
        most = jnp.int32(0)
        for e in range(experts):
            _, end, at = bounds(s, b, e)
            most = jnp.maximum(most, end - at)
        return jnp.maximum(most - 1, 0) // WINDOW

    def put_rows(s, e, at, begin, new, gates):
        head = pl.ds(pl.multiple_of(e * stride + at, 16), 16)
        rest = pl.ds(pl.multiple_of(e * stride + at + 16, 16), WINDOW - 16)
        old = lax.broadcasted_iota(jnp.int32, (16, 1), 0) + at < begin
        rows_ref[s, head, :] = jnp.where(old, rows_ref[s, head, :].astype(jnp.float32), new[:16]).astype(jnp.bfloat16)
        row_gate[s, head, :] = jnp.where(old, row_gate[s, head, :], gates[:16])
        rows_ref[s, rest, :] = new[16:].astype(jnp.bfloat16)
        row_gate[s, rest, :] = gates[16:]

    def dispatch(i, _):
        s, b = i // blocks, lax.rem(i, blocks)
        span = pl.ds(pl.multiple_of(b * BLOCK, BLOCK), BLOCK)
        local = lax.broadcasted_iota(jnp.int32, (WINDOW, BLOCK), 0)

        def one_hot(e, at):
            return (local + at).astype(jnp.float32) == slot_lane[s, e:e + 1, span]

        def gates_of(pick, e):
            return jnp.sum(jnp.where(pick, gate_lane[s, e:e + 1, span], 0.0), axis=1, keepdims=True)

        gates = []
        for e in range(experts):
            _, _, at = bounds(s, b, e)
            pick = one_hot(e, at)
            gates.append(gates_of(pick, e))
            pick_ref[e * WINDOW:(e + 1) * WINDOW, :] = pick.astype(jnp.bfloat16)
        new = jnp.dot(pick_ref[...], tok_ref[s, span, :], preferred_element_type=jnp.float32)
        for e in range(experts):
            begin, _, at = bounds(s, b, e)
            put_rows(s, e, at, begin, new[e * WINDOW:(e + 1) * WINDOW, :], gates[e])

        def more(j, _):
            k, e = j // experts + 1, lax.rem(j, experts)
            begin, _, at = bounds(s, b, e)
            at = at + k * WINDOW

            @pl.when(at < jnp.minimum(base_ref[s, b + 1, e], cap))
            def _():
                pick = (local + at).astype(jnp.float32) == slot_lane[s, pl.ds(e, 1), span]
                got = jnp.sum(jnp.where(pick, gate_lane[s, pl.ds(e, 1), span], 0.0), axis=1, keepdims=True)
                new = jnp.dot(pick.astype(jnp.bfloat16), tok_ref[s, span, :], preferred_element_type=jnp.float32)
                put_rows(s, e, at, begin, new, got)

            return 0

        lax.fori_loop(0, extra_windows(s, b) * experts, more, 0)
        return 0

    lax.fori_loop(0, sources * blocks, dispatch, 0)

    def tile(e, s, buf, lo, rows):
        where = pl.ds(pl.multiple_of(e * stride + lo, 16), rows)
        x = rows_ref[s, where, :]
        for at, width in chunks_of(ff, CHUNK):
            a = jnp.dot(x, wg_buf[buf, :, at:at + width], preferred_element_type=jnp.float32)
            b = jnp.dot(x, wu_buf[buf, :, at:at + width], preferred_element_type=jnp.float32)
            h_ref[:rows, at:at + width] = (a * jax.nn.sigmoid(a) * b).astype(jnp.bfloat16)
        y = jnp.dot(h_ref[:rows, :], wd_buf[buf], preferred_element_type=jnp.float32)
        rows_ref[s, where, :] = (y * row_gate[s, where, :]).astype(jnp.bfloat16)

    def expert_step(e, _):
        buf = lax.rem(e, 2)
        for copy in weight_copies(e, buf):
            copy.wait()

        @pl.when(e + 1 < experts)
        def _():
            for copy in weight_copies(e + 1, 1 - buf):
                copy.start()

        def source_step(s, _):
            n = jnp.minimum(base_ref[s, blocks, e], cap)

            @pl.when((n > 0) & (n <= small))
            def _():
                tile(e, s, buf, 0, small)

            @pl.when(n > small)
            def _():
                tile(e, s, buf, 0, cap)

            return 0

        lax.fori_loop(0, sources, source_step, 0)
        return 0

    lax.fori_loop(0, experts, expert_step, 0)

    def gather_rows(i, y_ref):
        s, b = i // blocks, lax.rem(i, blocks)
        span = pl.ds(pl.multiple_of(b * BLOCK, BLOCK), BLOCK)
        local = lax.broadcasted_iota(jnp.int32, (BLOCK, WINDOW), 1)
        puts = []
        for e in range(experts):
            _, _, at = bounds(s, b, e)
            puts.append(((local + at).astype(jnp.float32) == slot_sub[s, span, e:e + 1]).astype(jnp.bfloat16))
            y_ref[e * WINDOW:(e + 1) * WINDOW, :] = rows_ref[s, pl.ds(pl.multiple_of(e * stride + at, 16), WINDOW), :]
        return jnp.concatenate(puts, axis=1)

    def combine(i, put, y_ref):
        s, b = i // blocks, lax.rem(i, blocks)
        span = pl.ds(pl.multiple_of(b * BLOCK, BLOCK), BLOCK)
        total = jnp.dot(put, y_ref[...], preferred_element_type=jnp.float32)
        tok_ref[s, span, :] = total.astype(jnp.bfloat16)
        if adds:
            acc_ref[...] = total

    def finish(i):
        s, b = i // blocks, lax.rem(i, blocks)
        span = pl.ds(pl.multiple_of(b * BLOCK, BLOCK), BLOCK)
        local = lax.broadcasted_iota(jnp.int32, (BLOCK, WINDOW), 1)
        extra = extra_windows(s, b)

        @pl.when(extra > 0)
        def _():
            acc_ref[...] = jnp.zeros_like(acc_ref)

            def every(i, _):
                k, e = i // experts, lax.rem(i, experts)
                _, _, at = bounds(s, b, e)
                at = at + k * WINDOW

                @pl.when(at < jnp.minimum(base_ref[s, b + 1, e], cap))
                def _():
                    col = lax.broadcasted_iota(jnp.int32, (BLOCK, experts), 1)
                    mine = jnp.sum(jnp.where(col == e, slot_sub[s, span, :], 0.0), axis=1, keepdims=True)
                    put = ((local + at).astype(jnp.float32) == mine).astype(jnp.bfloat16)
                    y = rows_ref[s, pl.ds(pl.multiple_of(e * stride + at, 16), WINDOW), :]
                    acc_ref[...] += jnp.dot(put, y, preferred_element_type=jnp.float32)

                return 0

            lax.fori_loop(0, (extra + 1) * experts, every, 0)
            tok_ref[s, span, :] = acc_ref[...].astype(jnp.bfloat16)

        if adds:

            @pl.when(s == 0)
            def _():
                rows = acc_ref[...]
                for k in range(adds):
                    rows += add_ref[k, span, :].astype(jnp.float32)
                sum_ref[span, :] = rows
                pltpu.make_async_copy(sum_ref.at[span, :], out_hbm[0].at[span, :], out_sem).start()

        for t in range(1 if adds else 0, sources):

            @pl.when(s == t)
            def _():
                pltpu.make_async_copy(tok_ref.at[t, span, :], out_hbm[t].at[span, :], out_sem).start()

    if adds:
        for copy in add_copies:
            copy.wait()

    def pair(j, _):
        put_a = gather_rows(2 * j, yblk_ref)
        put_b = gather_rows(2 * j + 1, yblk2_ref)
        combine(2 * j, put_a, yblk_ref)
        if adds:
            finish(2 * j)
        combine(2 * j + 1, put_b, yblk2_ref)
        if not adds:
            finish(2 * j)
        finish(2 * j + 1)
        return 0

    lax.fori_loop(0, sources * blocks // 2, pair, 0)
    for s in range(sources):
        src = sum_ref if adds and s == 0 else tok_ref.at[s]
        pltpu.make_async_copy(src, out_hbm[s], out_sem).wait()


def phase(routes, toks, wg, wu, wd, cap, first=0, experts=None, adds=(), after=()):
    sources, _, tok_dev = routes.shape
    d_model = toks[0].shape[1]
    ff = wg.shape[2]
    experts = experts or wg.shape[0]
    small = min(cap, 256)
    vm = pl.BlockSpec(memory_space=pltpu.VMEM)
    hbm = pl.BlockSpec(memory_space=pl.ANY)
    blocks = tok_dev // BLOCK
    height = experts * (cap + WINDOW)
    sum_scratch = [
        pltpu.VMEM((len(adds), tok_dev, d_model), jnp.bfloat16),
        pltpu.VMEM((tok_dev, d_model), jnp.float32),
        pltpu.SemaphoreType.DMA((len(adds),)),
    ] if adds else []
    return pl.pallas_call(
        functools.partial(phase_kernel, cap, small, first, experts, len(toks), len(adds), len(after)),
        out_shape=[
            jax.ShapeDtypeStruct((tok_dev, d_model), jnp.float32 if adds and s == 0 else jnp.bfloat16) for s in range(sources)
        ],
        in_specs=[vm] + [hbm] * (len(toks) + 3 + len(adds) + len(after)),
        out_specs=[hbm] * sources,
        scratch_shapes=[
            pltpu.VMEM((2, d_model, ff), jnp.bfloat16),
            pltpu.VMEM((2, d_model, ff), jnp.bfloat16),
            pltpu.VMEM((2, ff, d_model), jnp.bfloat16),
            pltpu.VMEM((sources, tok_dev, d_model), jnp.bfloat16),
            pltpu.VMEM((sources, height, d_model), jnp.bfloat16),
            pltpu.VMEM((experts * WINDOW, BLOCK), jnp.bfloat16),
            pltpu.VMEM((experts * WINDOW, d_model), jnp.bfloat16),
            pltpu.VMEM((experts * WINDOW, d_model), jnp.bfloat16),
            pltpu.VMEM((BLOCK, d_model), jnp.float32),
            pltpu.VMEM((sources, experts, tok_dev), jnp.float32),
            pltpu.VMEM((sources, experts, tok_dev), jnp.float32),
            pltpu.VMEM((sources, tok_dev, experts), jnp.float32),
            pltpu.VMEM((sources, height, 1), jnp.float32),
            pltpu.VMEM((cap, ff), jnp.bfloat16),
            pltpu.SMEM((sources, blocks + 1, experts), jnp.int32),
            pltpu.SemaphoreType.DMA((2, 3 * PARTS)),
            pltpu.SemaphoreType.DMA((len(toks),)),
            pltpu.SemaphoreType.DMA,
        ] + sum_scratch,
        compiler_params=pltpu.CompilerParams(vmem_limit_bytes=60 * 2**20),
        cost_estimate=pl.CostEstimate(
            flops=6 * sources * experts * small * d_model * ff,
            bytes_accessed=6 * experts * d_model * ff,
            transcendentals=0,
        ),
        name="moe_phase",
    )(routes, *toks, wg, wu, wd, *adds, *after)


def solution(mesh):
    ep_size = mesh.shape["ep"]
    tp_size = mesh.shape["tp"]
    row_spec = P(("dp", "ep", "tp"), None)
    axes = ("dp", "ep", "tp")
    ranks = [(d, y, t) for d in range(mesh.shape["dp"]) for y in range(ep_size) for t in range(tp_size)]

    def rank_of(d, y, t):
        return (d * ep_size + y) * tp_size + t

    def shift(arr, flip_ep, flip_tp):
        return lax.ppermute(arr, axes, [(rank_of(*r), rank_of(r[0], r[1] ^ flip_ep, r[2] ^ flip_tp)) for r in ranks])

    def local_layer(tokens, expert_ids, gates, w_gate, w_up, w_down):
        tok_dev, _ = tokens.shape
        top_k = expert_ids.shape[1]
        local_experts = w_gate.shape[0]
        capacity = 5 * top_k * tok_dev // (4 * local_experts * ep_size)
        first = (lax.axis_index("ep") * local_experts).astype(jnp.float32)
        routes = jnp.concatenate([expert_ids.T.astype(jnp.float32), gates.T], axis=0)

        def run(tok_list, route_list, after=(), **part):
            stacked = jnp.stack(route_list)
            lines = jnp.arange(2 * top_k)[None, :, None] < top_k
            stacked = jnp.where(lines, stacked - first, stacked)
            return phase(stacked, tok_list, w_gate, w_up, w_down, capacity, after=after, **part)

        t_p, r_p = shift(tokens, 0, 1), shift(routes, 0, 1)
        r_x, r_y, t_x, t_y = shift(routes, 0, 2), shift(routes, 1, 0), shift(tokens, 0, 2), shift(tokens, 1, 0)
        own, own_p = run([tokens, t_p], [routes, r_p], experts=local_experts // 2)
        p_back = shift(own_p, 0, 1)
        r_x, r_y, t_x, t_y, own = lax.optimization_barrier((r_x, r_y, t_x, t_y, own))
        r_xp, t_xp = shift(r_x, 0, 1), shift(t_x, 0, 1)
        r_yp, t_yp = shift(r_y, 0, 1), shift(t_y, 0, 1)
        r_d, t_d = shift(r_x, 1, 0), shift(t_x, 1, 0)
        x_a, x_b = run([t_x, t_xp], [r_x, r_xp], after=(own,))
        x_back = shift(x_a, 0, 2)
        xp_back = shift(x_b, 0, 3)
        r_d, t_d, _ = lax.optimization_barrier((r_d, t_d, x_a))
        r_dp, t_dp = shift(r_d, 0, 1), shift(t_d, 0, 1)
        y_a, y_b = run([t_y, t_yp], [r_y, r_yp], after=(x_a,))
        y_back = shift(y_a, 1, 0)
        yp_back = shift(y_b, 1, 1)
        d_a, d_b = run([t_d, t_dp], [r_d, r_dp], after=(y_a,))
        d_in = shift(d_b, 0, 1)
        d_sum = add_pair(d_a, d_in)
        d_back = shift(d_sum, 1, 2)
        rest, rest_p = run(
            [tokens, t_p],
            [routes, r_p],
            after=(d_sum,),
            first=local_experts // 2,
            experts=local_experts // 2,
            adds=(own, p_back, x_back, xp_back, y_back, yp_back),
        )
        rest_back = shift(rest_p, 0, 1)
        total = rest + rest_back.astype(jnp.float32) + d_back.astype(jnp.float32)
        return total.astype(jnp.bfloat16)

    return jax.shard_map(
        local_layer,
        mesh=mesh,
        in_specs=(row_spec, row_spec, row_spec, P("ep", None, "tp"), P("ep", None, "tp"), P("ep", "tp", None)),
        out_specs=row_spec,
        check_vma=False,
    )
```

profile of v0, /device:TPU:0, one launch (start us, length us, event | category | flops | bytes accessed | tf_op | source)
XLA Modules:
  0.0 461.3 jit_solution(13848041119164114590)
XLA Ops:
  0.0 0.8 collective-permute-start.1
  0.8 0.7 convert_bitcast_fusion
  1.6 0.7 fusion
  2.3 0.0 collective-permute-start
  2.3 3.0 collective-permute-start.2
  5.3 1.5 collective-permute-start.3
  6.8 0.5 collective-permute-start.4
  7.4 0.0 collective-permute-done
  7.4 0.0 collective-permute-start.5
  7.4 0.7 subtract_select_fusion.3.route_ref
  8.1 0.0 collective-permute-done.1.refs_1_
  8.1 1.2 copy-done.1
  9.2 41.2 %moe_phase.5 = (bf16[1024,768]{1,0:T(8,128)(2,1)}, bf16[1024,768]{1,0:T(8,128)(2,1)}) custom-call(f32[2,8,1024]{2,1,0:T(8,128)} %subtract_select_fusion.3.route_ref, bf16[1024,768]{1,0:T(8,128)(2,1)} %refs_0_.3, bf16[1024,768]{1,0:T(8,128)(2,1)} %copy-done.1, bf16[8,768,2688]{2,1,0:T(8,128)(2,1)} %refs_2_.9, bf16[8,768,2688]{2,1,0:T(8,128)(2,1)} %refs_3_.9, ...), custom_call_target="tpu_custom_call" | custom-call | flops 25367150592 | bytes 49545216 | tf_op jit(solution)/shard_map/moe_phase/pallas_call | solution.py:299
  50.5 0.0 collective-permute-done.3
  50.5 0.0 copy-start.3
  50.5 0.0 collective-permute-done.5.refs_0_
  50.5 0.0 collective-permute-start.8
  50.6 0.5 collective-permute-start.7
  51.1 0.0 collective-permute-start.11
  51.1 4.7 %collective-permute-start.16 = (bf16[1024,768]{1,0:T(8,128)(2,1)S(1)}, bf16[1024,768]{1,0:T(8,128)(2,1)S(1)}, u32[]{:S(2)}, u32[]{:S(2)}) collective-permute-start(bf16[1024,768]{1,0:T(8,128)(2,1)S(1)} %collective-permute-done.4.refs_0_), channel_id=1, source_target_pairs={{0,4},{1,5},{2,6},{3,7},{4,0},{5,1},{6,2},{7,3}} | collective-permute-start | bytes 4718600 | tf_op jit(solution)/shard_map/ppermute | solution.py:347
  55.8 0.0 collective-permute-start.15
  55.8 0.2 collective-permute-start.12
  56.0 0.0 collective-permute-done.11
  56.0 0.7 subtract_select_fusion.1
  56.7 1.2 copy-done.5
  57.9 78.4 %moe_phase.6 = (bf16[1024,768]{1,0:T(8,128)(2,1)}, bf16[1024,768]{1,0:T(8,128)(2,1)}) custom-call(f32[2,8,1024]{2,1,0:T(8,128)} %get-tuple-element.42.route_ref, bf16[1024,768]{1,0:T(8,128)(2,1)} %copy-done.3, bf16[1024,768]{1,0:T(8,128)(2,1)} %copy-done.5, bf16[8,768,2688]{2,1,0:T(8,128)(2,1)} %refs_2_.9, bf16[8,768,2688]{2,1,0:T(8,128)(2,1)} %refs_3_.9, ...), custom_call_target="tpu_custom_call" | custom-call | flops 50734301184 | bytes 99090432 | tf_op jit(solution)/shard_map/moe_phase/pallas_call | solution.py:299
  136.4 0.0 copy-start.4
  136.4 0.3 collective-permute-start.18
  136.8 0.2 collective-permute-start.17
  137.0 73.9 %moe_phase.7 = (bf16[1024,768]{1,0:T(8,128)(2,1)}, bf16[1024,768]{1,0:T(8,128)(2,1)}) custom-call(f32[2,8,1024]{2,1,0:T(8,128)} %get-tuple-element.41.route_ref, bf16[1024,768]{1,0:T(8,128)(2,1)} %collective-permute-done.5.refs_0_, bf16[1024,768]{1,0:T(8,128)(2,1)} %collective-permute-done.12.refs_1_, bf16[8,768,2688]{2,1,0:T(8,128)(2,1)} %refs_2_.9, ...), custom_call_target="tpu_custom_call" | custom-call | flops 50734301184 | bytes 99090432 | tf_op jit(solution)/shard_map/moe_phase/pallas_call | solution.py:299
  210.9 0.7 subtract_select_fusion.route_ref
  211.6 1.2 copy-done.6
  212.8 78.6 %moe_phase.8 = (bf16[1024,768]{1,0:T(8,128)(2,1)}, bf16[1024,768]{1,0:T(8,128)(2,1)}) custom-call(f32[2,8,1024]{2,1,0:T(8,128)} %subtract_select_fusion.route_ref, bf16[1024,768]{1,0:T(8,128)(2,1)} %copy-done.4, bf16[1024,768]{1,0:T(8,128)(2,1)} %copy-done.6, bf16[8,768,2688]{2,1,0:T(8,128)(2,1)} %refs_2_.9, bf16[8,768,2688]{2,1,0:T(8,128)(2,1)} %refs_3_.9, ...), custom_call_target="tpu_custom_call" | custom-call | flops 50734301184 | bytes 99090432 | tf_op jit(solution)/shard_map/moe_phase/pallas_call | solution.py:299
  291.4 0.3 collective-permute-start.19
  291.8 0.2 collective-permute-start.6
  292.0 7.3 %collective-permute-start.13 = (bf16[1024,768]{1,0:T(8,128)(2,1)}, bf16[1024,768]{1,0:T(8,128)(2,1)}, u32[]{:S(2)}, u32[]{:S(2)}) collective-permute-start(bf16[1024,768]{1,0:T(8,128)(2,1)} %get-tuple-element.31.refs_5_), channel_id=1, source_target_pairs={{0,4},{1,5},{2,6},{3,7},{4,0},{5,1},{6,2},{7,3}} | collective-permute-start | bytes 4718600 | tf_op jit(solution)/shard_map/ppermute | solution.py:347
  299.3 3.4 collective-permute-start.10
  302.7 0.3 collective-permute-start.9
  303.0 3.0 add_convert_fusion.1.refs_11_
  306.1 28.8 %collective-permute-done.13.refs_9_ = bf16[1024,768]{1,0:T(8,128)(2,1)} collective-permute-done((bf16[1024,768]{1,0:T(8,128)(2,1)}, bf16[1024,768]{1,0:T(8,128)(2,1)}, u32[]{:S(2)}, u32[]{:S(2)}) %collective-permute-start.13) | collective-permute-done | bytes 1572896 | tf_op jit(solution)/shard_map/ppermute | solution.py:347
  334.9 33.0 %collective-permute-done.14.refs_10_ = bf16[1024,768]{1,0:T(8,128)(2,1)} collective-permute-done((bf16[1024,768]{1,0:T(8,128)(2,1)}, bf16[1024,768]{1,0:T(8,128)(2,1)}, u32[]{:S(2)}, u32[]{:S(2)}) %collective-permute-start.14) | collective-permute-done | bytes 1572896 | tf_op jit(solution)/shard_map/ppermute | solution.py:347
  367.9 3.8 collective-permute-done.9.refs_7_
  371.7 47.7 %moe_phase.9 = (f32[1024,768]{1,0:T(8,128)}, bf16[1024,768]{1,0:T(8,128)(2,1)}) custom-call(f32[2,8,1024]{2,1,0:T(8,128)} %subtract_select_fusion.3.route_ref, bf16[1024,768]{1,0:T(8,128)(2,1)} %refs_0_.3, bf16[1024,768]{1,0:T(8,128)(2,1)} %copy-done.1, bf16[8,768,2688]{2,1,0:T(8,128)(2,1)} %refs_2_.9, bf16[8,768,2688]{2,1,0:T(8,128)(2,1)} %refs_3_.9, ...), custom_call_target="tpu_custom_call" | custom-call | flops 25367150592 | bytes 49545216 | tf_op jit(solution)/shard_map/moe_phase/pallas_call | solution.py:299
  419.4 0.0 collective-permute-start.20
  419.5 3.1 collective-permute-start.21
  422.6 0.5 collective-permute-done.20
  423.1 34.6 %collective-permute-done.21 = bf16[1024,768]{1,0:T(8,128)(2,1)S(1)} collective-permute-done((bf16[1024,768]{1,0:T(8,128)(2,1)S(1)}, bf16[1024,768]{1,0:T(8,128)(2,1)S(1)}, u32[]{:S(2)}, u32[]{:S(2)}) %collective-permute-start.21) | collective-permute-done | bytes 1572896 | tf_op jit(solution)/shard_map/ppermute | solution.py:347
  457.6 3.5 add_convert_fusion
  (23 shorter events, 0.1 us)
Async XLA Ops:
  0.0 8.1 %collective-permute-start.1 = (bf16[1024,768]{1,0:T(8,128)(2,1)}, bf16[1024,768]{1,0:T(8,128)(2,1)S(1)}, u32[]{:S(2)}, u32[]{:S(2)}) collective-permute-start(bf16[1024,768]{1,0:T(8,128)(2,1)} %refs_0_.3), channel_id=1, source_target_pairs={{0,1},{1,0},{2,3},{3,2},{4,5},{5,4},{6,7},{7,6}} | collective-permute-start | bytes 4718600 | tf_op jit(solution)/shard_map/ppermute | solution.py:347
  2.3 5.1 %collective-permute-start = (f32[8,1024]{1,0:T(8,128)S(1)}, f32[8,1024]{1,0:T(8,128)S(1)}, u32[]{:S(2)}, u32[]{:S(2)}) collective-permute-start(f32[8,1024]{1,0:T(8,128)S(1)} %get-tuple-element.40), channel_id=1, source_target_pairs={{0,1},{1,0},{2,3},{3,2},{4,5},{5,4},{6,7},{7,6}} | collective-permute-start | bytes 98312 | tf_op jit(solution)/shard_map/ppermute | solution.py:347
  2.3 48.2 %collective-permute-start.2 = (f32[8,1024]{1,0:T(8,128)S(1)}, f32[8,1024]{1,0:T(8,128)S(1)}, u32[]{:S(2)}, u32[]{:S(2)}) collective-permute-start(f32[8,1024]{1,0:T(8,128)S(1)} %get-tuple-element.40), channel_id=1, source_target_pairs={{0,2},{1,3},{2,0},{3,1},{4,6},{5,7},{6,4},{7,5}} | collective-permute-start | bytes 98312 | tf_op jit(solution)/shard_map/ppermute | solution.py:347
  5.3 45.2 %collective-permute-start.3 = (f32[8,1024]{1,0:T(8,128)S(1)}, f32[8,1024]{1,0:T(8,128)S(1)}, u32[]{:S(2)}, u32[]{:S(2)}) collective-permute-start(f32[8,1024]{1,0:T(8,128)S(1)} %get-tuple-element.40), channel_id=1, source_target_pairs={{0,4},{1,5},{2,6},{3,7},{4,0},{5,1},{6,2},{7,3}} | collective-permute-start | bytes 98312 | tf_op jit(solution)/shard_map/ppermute | solution.py:347
  6.8 43.7 %collective-permute-start.4 = (bf16[1024,768]{1,0:T(8,128)(2,1)}, bf16[1024,768]{1,0:T(8,128)(2,1)S(1)}, u32[]{:S(2)}, u32[]{:S(2)}) collective-permute-start(bf16[1024,768]{1,0:T(8,128)(2,1)} %refs_0_.3), channel_id=1, source_target_pairs={{0,2},{1,3},{2,0},{3,1},{4,6},{5,7},{6,4},{7,5}} | collective-permute-start | bytes 4718600 | tf_op jit(solution)/shard_map/ppermute | solution.py:347
  7.4 43.2 %collective-permute-start.5 = (bf16[1024,768]{1,0:T(8,128)(2,1)}, bf16[1024,768]{1,0:T(8,128)(2,1)}, u32[]{:S(2)}, u32[]{:S(2)}) collective-permute-start(bf16[1024,768]{1,0:T(8,128)(2,1)} %refs_0_.3), channel_id=1, source_target_pairs={{0,4},{1,5},{2,6},{3,7},{4,0},{5,1},{6,2},{7,3}} | collective-permute-start | bytes 4718600 | tf_op jit(solution)/shard_map/ppermute | solution.py:347
  8.1 1.2 copy-start.1
  50.5 7.4 %copy-start.3 = (bf16[1024,768]{1,0:T(8,128)(2,1)}, bf16[1024,768]{1,0:T(8,128)(2,1)S(1)}, u32[]{:S(2)}) copy-start(bf16[1024,768]{1,0:T(8,128)(2,1)S(1)} %collective-permute-done.4.refs_0_) | copy-start | bytes 4718596
  50.5 6.2 %collective-permute-start.8 = (bf16[1024,768]{1,0:T(8,128)(2,1)S(1)}, bf16[1024,768]{1,0:T(8,128)(2,1)S(1)}, u32[]{:S(2)}, u32[]{:S(2)}) collective-permute-start(bf16[1024,768]{1,0:T(8,128)(2,1)S(1)} %collective-permute-done.4.refs_0_), channel_id=1, source_target_pairs={{0,1},{1,0},{2,3},{3,2},{4,5},{5,4},{6,7},{7,6}} | collective-permute-start | bytes 4718600 | tf_op jit(solution)/shard_map/ppermute | solution.py:347
  50.6 5.2 %collective-permute-start.7 = (f32[8,1024]{1,0:T(8,128)S(1)}, f32[8,1024]{1,0:T(8,128)S(1)}, u32[]{:S(2)}, u32[]{:S(2)}) collective-permute-start(f32[8,1024]{1,0:T(8,128)S(1)} %collective-permute-done.2), channel_id=1, source_target_pairs={{0,1},{1,0},{2,3},{3,2},{4,5},{5,4},{6,7},{7,6}} | collective-permute-start | bytes 98312 | tf_op jit(solution)/shard_map/ppermute | solution.py:347
  51.1 4.9 %collective-permute-start.11 = (f32[8,1024]{1,0:T(8,128)S(1)}, f32[8,1024]{1,0:T(8,128)S(1)}, u32[]{:S(2)}, u32[]{:S(2)}) collective-permute-start(f32[8,1024]{1,0:T(8,128)S(1)} %collective-permute-done.3), channel_id=1, source_target_pairs={{0,1},{1,0},{2,3},{3,2},{4,5},{5,4},{6,7},{7,6}} | collective-permute-start | bytes 98312 | tf_op jit(solution)/shard_map/ppermute | solution.py:347
  51.1 85.3 %collective-permute-start.16 = (bf16[1024,768]{1,0:T(8,128)(2,1)S(1)}, bf16[1024,768]{1,0:T(8,128)(2,1)S(1)}, u32[]{:S(2)}, u32[]{:S(2)}) collective-permute-start(bf16[1024,768]{1,0:T(8,128)(2,1)S(1)} %collective-permute-done.4.refs_0_), channel_id=1, source_target_pairs={{0,4},{1,5},{2,6},{3,7},{4,0},{5,1},{6,2},{7,3}} | collective-permute-start | bytes 4718600 | tf_op jit(solution)/shard_map/ppermute | solution.py:347
  55.8 80.6 %collective-permute-start.15 = (f32[8,1024]{1,0:T(8,128)S(1)}, f32[8,1024]{1,0:T(8,128)S(1)}, u32[]{:S(2)}, u32[]{:S(2)}) collective-permute-start(f32[8,1024]{1,0:T(8,128)S(1)} %collective-permute-done.2), channel_id=1, source_target_pairs={{0,4},{1,5},{2,6},{3,7},{4,0},{5,1},{6,2},{7,3}} | collective-permute-start | bytes 98312 | tf_op jit(solution)/shard_map/ppermute | solution.py:347
  55.8 81.2 %collective-permute-start.12 = (bf16[1024,768]{1,0:T(8,128)(2,1)}, bf16[1024,768]{1,0:T(8,128)(2,1)}, u32[]{:S(2)}, u32[]{:S(2)}) collective-permute-start(bf16[1024,768]{1,0:T(8,128)(2,1)} %collective-permute-done.5.refs_0_), channel_id=1, source_target_pairs={{0,1},{1,0},{2,3},{3,2},{4,5},{5,4},{6,7},{7,6}} | collective-permute-start | bytes 4718600 | tf_op jit(solution)/shard_map/ppermute | solution.py:347
  56.7 1.2 copy-start.5
  136.4 74.5 %copy-start.4 = (bf16[1024,768]{1,0:T(8,128)(2,1)}, bf16[1024,768]{1,0:T(8,128)(2,1)S(1)}, u32[]{:S(2)}) copy-start(bf16[1024,768]{1,0:T(8,128)(2,1)S(1)} %collective-permute-done.16.refs_0_) | copy-start | bytes 4718596
  136.4 75.2 %collective-permute-start.18 = (bf16[1024,768]{1,0:T(8,128)(2,1)S(1)}, bf16[1024,768]{1,0:T(8,128)(2,1)S(1)}, u32[]{:S(2)}, u32[]{:S(2)}) collective-permute-start(bf16[1024,768]{1,0:T(8,128)(2,1)S(1)} %collective-permute-done.16.refs_0_), channel_id=1, source_target_pairs={{0,1},{1,0},{2,3},{3,2},{4,5},{5,4},{6,7},{7,6}} | collective-permute-start | bytes 4718600 | tf_op jit(solution)/shard_map/ppermute | solution.py:347
  136.8 74.2 %collective-permute-start.17 = (f32[8,1024]{1,0:T(8,128)S(1)}, f32[8,1024]{1,0:T(8,128)S(1)}, u32[]{:S(2)}, u32[]{:S(2)}) collective-permute-start(f32[8,1024]{1,0:T(8,128)S(1)} %collective-permute-done.15), channel_id=1, source_target_pairs={{0,1},{1,0},{2,3},{3,2},{4,5},{5,4},{6,7},{7,6}} | collective-permute-start | bytes 98312 | tf_op jit(solution)/shard_map/ppermute | solution.py:347
  211.6 1.2 copy-start.6
  291.4 11.3 %collective-permute-start.19 = (bf16[1024,768]{1,0:T(8,128)(2,1)}, bf16[1024,768]{1,0:T(8,128)(2,1)S(1)}, u32[]{:S(2)}, u32[]{:S(2)}) collective-permute-start(bf16[1024,768]{1,0:T(8,128)(2,1)} %get-tuple-element.36), channel_id=1, source_target_pairs={{0,1},{1,0},{2,3},{3,2},{4,5},{5,4},{6,7},{7,6}} | collective-permute-start | bytes 4718600 | tf_op jit(solution)/shard_map/ppermute | solution.py:347
  291.8 14.3 %collective-permute-start.6 = (bf16[1024,768]{1,0:T(8,128)(2,1)}, bf16[1024,768]{1,0:T(8,128)(2,1)S(1)}, u32[]{:S(2)}, u32[]{:S(2)}) collective-permute-start(bf16[1024,768]{1,0:T(8,128)(2,1)} %get-tuple-element.24), channel_id=1, source_target_pairs={{0,1},{1,0},{2,3},{3,2},{4,5},{5,4},{6,7},{7,6}} | collective-permute-start | bytes 4718600 | tf_op jit(solution)/shard_map/ppermute | solution.py:347
  292.0 42.9 %collective-permute-start.13 = (bf16[1024,768]{1,0:T(8,128)(2,1)}, bf16[1024,768]{1,0:T(8,128)(2,1)}, u32[]{:S(2)}, u32[]{:S(2)}) collective-permute-start(bf16[1024,768]{1,0:T(8,128)(2,1)} %get-tuple-element.31.refs_5_), channel_id=1, source_target_pairs={{0,4},{1,5},{2,6},{3,7},{4,0},{5,1},{6,2},{7,3}} | collective-permute-start | bytes 4718600 | tf_op jit(solution)/shard_map/ppermute | solution.py:347
  299.3 68.6 %collective-permute-start.14 = (bf16[1024,768]{1,0:T(8,128)(2,1)}, bf16[1024,768]{1,0:T(8,128)(2,1)}, u32[]{:S(2)}, u32[]{:S(2)}) collective-permute-start(bf16[1024,768]{1,0:T(8,128)(2,1)} %get-tuple-element.32), channel_id=1, source_target_pairs={{0,5},{1,4},{2,7},{3,6},{4,1},{5,0},{6,3},{7,2}} | collective-permute-start | bytes 4718600 | tf_op jit(solution)/shard_map/ppermute | solution.py:347
  299.3 68.6 %collective-permute-start.10 = (bf16[1024,768]{1,0:T(8,128)(2,1)}, bf16[1024,768]{1,0:T(8,128)(2,1)}, u32[]{:S(2)}, u32[]{:S(2)}) collective-permute-start(bf16[1024,768]{1,0:T(8,128)(2,1)} %get-tuple-element.28), channel_id=1, source_target_pairs={{0,3},{1,2},{2,1},{3,0},{4,7},{5,6},{6,5},{7,4}} | collective-permute-start | bytes 4718600 | tf_op jit(solution)/shard_map/ppermute | solution.py:347
  302.7 69.0 %collective-permute-start.9 = (bf16[1024,768]{1,0:T(8,128)(2,1)}, bf16[1024,768]{1,0:T(8,128)(2,1)}, u32[]{:S(2)}, u32[]{:S(2)}) collective-permute-start(bf16[1024,768]{1,0:T(8,128)(2,1)} %get-tuple-element.27.refs_5_), channel_id=1, source_target_pairs={{0,2},{1,3},{2,0},{3,1},{4,6},{5,7},{6,4},{7,5}} | collective-permute-start | bytes 4718600 | tf_op jit(solution)/shard_map/ppermute | solution.py:347
  306.1 113.4 %copy-start = (bf16[1024,768]{1,0:T(8,128)(2,1)S(1)}, bf16[1024,768]{1,0:T(8,128)(2,1)}, u32[]{:S(2)}) copy-start(bf16[1024,768]{1,0:T(8,128)(2,1)} %add_convert_fusion.1.refs_11_) | copy-start | bytes 4718596
  306.1 65.6 %copy-start.2 = (bf16[1024,768]{1,0:T(8,128)(2,1)}, bf16[1024,768]{1,0:T(8,128)(2,1)S(1)}, u32[]{:S(2)}) copy-start(bf16[1024,768]{1,0:T(8,128)(2,1)S(1)} %collective-permute-done.6.refs_6_) | copy-start | bytes 4718596
  419.4 3.6 collective-permute-start.20
  419.5 38.1 %collective-permute-start.21 = (bf16[1024,768]{1,0:T(8,128)(2,1)S(1)}, bf16[1024,768]{1,0:T(8,128)(2,1)S(1)}, u32[]{:S(2)}, u32[]{:S(2)}) collective-permute-start(bf16[1024,768]{1,0:T(8,128)(2,1)S(1)} %copy-done), channel_id=1, source_target_pairs={{0,6},{1,7},{2,4},{3,5},{4,2},{5,3},{6,0},{7,1}} | collective-permute-start | bytes 4718600 | tf_op jit(solution)/shard_map/ppermute | solution.py:347
where the time goes:
time: 470 us; the launch traced here: 461 us
  Pallas kernels  320 us (68%)
  waiting for transfers between devices  101 us (21%)
  starting transfers between devices  26.6 us (6%)
  other arithmetic  10.1 us (2%)
    pallas_call x5, Pallas kernels, phase(): pl.pallas_call(functools.partial(phase_kernel, cap, small, first, experts...  320 us
    ppermute x22, waiting for transfers between devices, shift(): lax.ppermute(arr, axes, [(rank_of(*r), rank_of(r[0], r[1] ^ flip_ep, r[2]...  101 us
    ppermute x22, starting transfers between devices, shift(): lax.ppermute(arr, axes, [(rank_of(*r), rank_of(r[0], r[1] ^ flip_ep, r[2]...  26.6 us
  transfers between devices with their start and end apart: 22, of which 5 were waited for; matrix products, arithmetic and copies ran while one was open for 1% of the time, Pallas kernels for 42%

commit v1 on v0

--- a/solution.py
+++ b/solution.py
@@ -29,21 +29,28 @@
     refs = refs[3 + adds + waits:]
     sources, lines, toks = route_ref.shape
     out_hbm = refs[:sources]
-    (wg_buf, wu_buf, wd_buf, tok_ref, rows_ref, pick_ref, yblk_ref, yblk2_ref, acc_ref, slot_lane, gate_lane, slot_sub, row_gate, h_ref,
+    (wg_buf, wu_buf, wx_buf, wd_buf, tok_ref, rows_ref, pick_ref, yblk_ref, yblk2_ref, acc_ref, slot_lane, gate_lane, slot_sub, row_gate, h_ref,
      base_ref, sems, tok_sems, out_sem, *sum_refs) = refs[sources:]
+    d_model = tok_ref.shape[2]
     top_k = lines // 2
     ff = wg_hbm.shape[2]
     blocks = toks // BLOCK
     stride = cap + WINDOW
+    main = wg_buf.shape[2]
 
     def weight_copies(e, buf):
-        copies = []
-        for i, (src, dst) in enumerate(((wg_hbm, wg_buf), (wu_hbm, wu_buf), (wd_hbm, wd_buf))):
-            rows = src.shape[1] // PARTS
-            for p in range(PARTS):
-                part = pl.ds(p * rows, rows)
-                copies.append(pltpu.make_async_copy(src.at[first + e, part, :], dst.at[buf, part, :], sems.at[buf, i * PARTS + p]))
-        return copies
+        at = first + e
+        pairs = []
+        for lo, rows in chunks_of(d_model, d_model // PARTS):
+            part = pl.ds(lo, rows)
+            pairs.append((wg_hbm.at[at, part, :main], wg_buf.at[buf, part, :]))
+            pairs.append((wu_hbm.at[at, part, :main], wu_buf.at[buf, part, :]))
+        if main < ff:
+            pairs.append((wg_hbm.at[at, :, main:], wx_buf.at[buf, :, :ff - main]))
+            pairs.append((wu_hbm.at[at, :, main:], wx_buf.at[buf, :, ff - main:]))
+        for lo, rows in chunks_of(ff, ff // PARTS):
+            pairs.append((wd_hbm.at[at, pl.ds(lo, rows), :], wd_buf.at[buf, pl.ds(lo, rows), :]))
+        return [pltpu.make_async_copy(src, dst, sems.at[buf, i]) for i, (src, dst) in enumerate(pairs)]
 
     size = sources * toks // pieces
     tok_copies = [
@@ -161,10 +168,14 @@
     def tile(e, s, buf, lo, rows):
         where = pl.ds(pl.multiple_of(e * stride + lo, 16), rows)
         x = rows_ref[s, where, :]
-        for at, width in chunks_of(ff, CHUNK):
+        for at, width in chunks_of(main, CHUNK):
             a = jnp.dot(x, wg_buf[buf, :, at:at + width], preferred_element_type=jnp.float32)
             b = jnp.dot(x, wu_buf[buf, :, at:at + width], preferred_element_type=jnp.float32)
             h_ref[:rows, at:at + width] = (a * jax.nn.sigmoid(a) * b).astype(jnp.bfloat16)
+        if main < ff:
+            ab = jnp.dot(x, wx_buf[buf], preferred_element_type=jnp.float32)
+            a, b = ab[:, :ff - main], ab[:, ff - main:]
+            h_ref[:rows, main:] = (a * jax.nn.sigmoid(a) * b).astype(jnp.bfloat16)
         y = jnp.dot(h_ref[:rows, :], wd_buf[buf], preferred_element_type=jnp.float32)
         rows_ref[s, where, :] = (y * row_gate[s, where, :]).astype(jnp.bfloat16)
 
@@ -181,14 +192,15 @@
         def source_step(s, _):
             n = jnp.minimum(base_ref[s, blocks, e], cap)
 
-            @pl.when((n > 0) & (n <= small))
+            @pl.when(n > 0)
             def _():
                 tile(e, s, buf, 0, small)
 
-            @pl.when(n > small)
-            def _():
-                tile(e, s, buf, 0, cap)
-
+            if cap > small:
+
+                @pl.when(n > small)
+                def _():
+                    tile(e, s, buf, small, cap - small)
             return 0
 
         lax.fori_loop(0, sources, source_step, 0)
@@ -285,6 +297,7 @@
     sources, _, tok_dev = routes.shape
     d_model = toks[0].shape[1]
     ff = wg.shape[2]
+    main = ff // 256 * 256
     experts = experts or wg.shape[0]
     small = min(cap, 256)
     vm = pl.BlockSpec(memory_space=pltpu.VMEM)
@@ -304,8 +317,9 @@
         in_specs=[vm] + [hbm] * (len(toks) + 3 + len(adds) + len(after)),
         out_specs=[hbm] * sources,
         scratch_shapes=[
-            pltpu.VMEM((2, d_model, ff), jnp.bfloat16),
-            pltpu.VMEM((2, d_model, ff), jnp.bfloat16),
+            pltpu.VMEM((2, d_model, main), jnp.bfloat16),
+            pltpu.VMEM((2, d_model, main), jnp.bfloat16),
+            pltpu.VMEM((2, d_model, 2 * max(ff - main, 128)), jnp.bfloat16),
             pltpu.VMEM((2, ff, d_model), jnp.bfloat16),
             pltpu.VMEM((sources, tok_dev, d_model), jnp.bfloat16),
             pltpu.VMEM((sources, height, d_model), jnp.bfloat16),
@@ -317,13 +331,13 @@
             pltpu.VMEM((sources, experts, tok_dev), jnp.float32),
             pltpu.VMEM((sources, tok_dev, experts), jnp.float32),
             pltpu.VMEM((sources, height, 1), jnp.float32),
-            pltpu.VMEM((cap, ff), jnp.bfloat16),
+            pltpu.VMEM((small, ff), jnp.bfloat16),
             pltpu.SMEM((sources, blocks + 1, experts), jnp.int32),
-            pltpu.SemaphoreType.DMA((2, 3 * PARTS)),
+            pltpu.SemaphoreType.DMA((2, 3 * PARTS + 2)),
             pltpu.SemaphoreType.DMA((len(toks),)),
             pltpu.SemaphoreType.DMA,
         ] + sum_scratch,
-        compiler_params=pltpu.CompilerParams(vmem_limit_bytes=60 * 2**20),
+        compiler_params=pltpu.CompilerParams(vmem_limit_bytes=67_000_000),
         cost_estimate=pl.CostEstimate(
             flops=6 * sources * experts * small * d_model * ff,
             bytes_accessed=6 * experts * d_model * ff,

time: 470 us -> 471 us (level)
  transfers between devices with their start and end apart: 22 -> 22, of which waited for: 5 -> 5; matrix products, arithmetic and copies ran while one was open for 1% -> 2% of each run, Pallas kernels for 42% -> 41%
where the time goes in v1:
time: 471 us; the launch traced here: 463 us
  Pallas kernels  319 us (68%)
  waiting for transfers between devices  101 us (21%)
  starting transfers between devices  31.1 us (7%)
  other arithmetic  11.6 us (2%)
    pallas_call x5, Pallas kernels, phase(): pl.pallas_call(functools.partial(phase_kernel, cap, small, first, experts...  319 us
    ppermute x22, waiting for transfers between devices, shift(): lax.ppermute(arr, axes, [(rank_of(*r), rank_of(r[0], r[1] ^ flip_ep, r[2]...  101 us
    ppermute x22, starting transfers between devices, shift(): lax.ppermute(arr, axes, [(rank_of(*r), rank_of(r[0], r[1] ^ flip_ep, r[2]...  31.1 us
  transfers between devices with their start and end apart: 22, of which 5 were waited for; matrix products, arithmetic and copies ran while one was open for 2% of the time, Pallas kernels for 41%

profile of v1, /device:TPU:0, one launch (start us, length us, event | category | flops | bytes accessed | tf_op | source)
XLA Modules:
  0.0 462.9 jit_solution(5476280323724084657)
XLA Ops:
  0.0 0.8 collective-permute-start.1
  0.8 0.7 convert_bitcast_fusion
  1.6 0.7 fusion
  2.3 0.0 collective-permute-start
  2.3 3.0 collective-permute-start.2
  5.3 1.5 collective-permute-start.3
  6.8 0.5 collective-permute-start.4
  7.4 0.0 collective-permute-done
  7.4 0.0 collective-permute-start.5
  7.4 0.7 subtract_select_fusion.3.route_ref
  8.1 0.0 collective-permute-done.1.refs_1_
  8.1 40.5 %moe_phase.5 = (bf16[1024,768]{1,0:T(8,128)(2,1)}, bf16[1024,768]{1,0:T(8,128)(2,1)}) custom-call(f32[2,8,1024]{2,1,0:T(8,128)} %subtract_select_fusion.3.route_ref, bf16[1024,768]{1,0:T(8,128)(2,1)} %refs_0_.3, bf16[1024,768]{1,0:T(8,128)(2,1)} %collective-permute-done.1.refs_1_, bf16[8,768,2688]{2,1,0:T(8,128)(2,1)} %refs_2_.9, ...), custom_call_target="tpu_custom_call" | custom-call | flops 25367150592 | bytes 49545216 | tf_op jit(solution)/shard_map/moe_phase/pallas_call | solution.py:312
  48.6 0.0 collective-permute-done.2
  48.6 0.0 collective-permute-done.4.refs_0_
  48.6 0.0 collective-permute-done.5.refs_0_
  48.6 0.0 collective-permute-start.8
  48.7 0.5 collective-permute-start.7
  49.2 0.0 collective-permute-start.11
  49.2 6.2 %collective-permute-start.16 = (bf16[1024,768]{1,0:T(8,128)(2,1)}, bf16[1024,768]{1,0:T(8,128)(2,1)}, u32[]{:S(2)}, u32[]{:S(2)}) collective-permute-start(bf16[1024,768]{1,0:T(8,128)(2,1)} %collective-permute-done.4.refs_0_), channel_id=1, source_target_pairs={{0,4},{1,5},{2,6},{3,7},{4,0},{5,1},{6,2},{7,3}} | collective-permute-start | bytes 4718600 | tf_op jit(solution)/shard_map/ppermute | solution.py:361
  55.4 0.0 collective-permute-start.15
  55.4 0.2 collective-permute-start.12
  55.6 0.0 collective-permute-done.11
  55.6 1.5 subtract_select_fusion.1
  57.1 0.0 collective-permute-done.8.refs_1_
  57.1 78.6 %moe_phase.6 = (bf16[1024,768]{1,0:T(8,128)(2,1)}, bf16[1024,768]{1,0:T(8,128)(2,1)}) custom-call(f32[2,8,1024]{2,1,0:T(8,128)} %get-tuple-element.42.route_ref, bf16[1024,768]{1,0:T(8,128)(2,1)} %collective-permute-done.4.refs_0_, bf16[1024,768]{1,0:T(8,128)(2,1)} %collective-permute-done.8.refs_1_, bf16[8,768,2688]{2,1,0:T(8,128)(2,1)} %refs_2_.9, ...), custom_call_target="tpu_custom_call" | custom-call | flops 50734301184 | bytes 99090432 | tf_op jit(solution)/shard_map/moe_phase/pallas_call | solution.py:312
  135.7 0.0 collective-permute-done.15
  135.7 0.0 collective-permute-done.16.refs_0_
  135.8 0.3 collective-permute-start.18
  136.1 0.2 collective-permute-start.17
  136.3 72.8 %moe_phase.7 = (bf16[1024,768]{1,0:T(8,128)(2,1)}, bf16[1024,768]{1,0:T(8,128)(2,1)}) custom-call(f32[2,8,1024]{2,1,0:T(8,128)} %get-tuple-element.41.route_ref, bf16[1024,768]{1,0:T(8,128)(2,1)} %collective-permute-done.5.refs_0_, bf16[1024,768]{1,0:T(8,128)(2,1)} %collective-permute-done.12.refs_1_, bf16[8,768,2688]{2,1,0:T(8,128)(2,1)} %refs_2_.9, ...), custom_call_target="tpu_custom_call" | custom-call | flops 50734301184 | bytes 99090432 | tf_op jit(solution)/shard_map/moe_phase/pallas_call | solution.py:312
  209.1 0.0 collective-permute-done.17
  209.1 1.5 subtract_select_fusion.route_ref
  210.6 78.4 %moe_phase.8 = (bf16[1024,768]{1,0:T(8,128)(2,1)}, bf16[1024,768]{1,0:T(8,128)(2,1)}) custom-call(f32[2,8,1024]{2,1,0:T(8,128)} %subtract_select_fusion.route_ref, bf16[1024,768]{1,0:T(8,128)(2,1)} %collective-permute-done.16.refs_0_, bf16[1024,768]{1,0:T(8,128)(2,1)} %collective-permute-done.18.refs_1_, bf16[8,768,2688]{2,1,0:T(8,128)(2,1)} %refs_2_.9, ...), custom_call_target="tpu_custom_call" | custom-call | flops 50734301184 | bytes 99090432 | tf_op jit(solution)/shard_map/moe_phase/pallas_call | solution.py:312
  289.0 0.3 collective-permute-start.19
  289.4 0.2 collective-permute-start.6
  289.6 9.1 %collective-permute-start.13 = (bf16[1024,768]{1,0:T(8,128)(2,1)}, bf16[1024,768]{1,0:T(8,128)(2,1)}, u32[]{:S(2)}, u32[]{:S(2)}) collective-permute-start(bf16[1024,768]{1,0:T(8,128)(2,1)} %get-tuple-element.31.refs_5_), channel_id=1, source_target_pairs={{0,4},{1,5},{2,6},{3,7},{4,0},{5,1},{6,2},{7,3}} | collective-permute-start | bytes 4718600 | tf_op jit(solution)/shard_map/ppermute | solution.py:361
  298.7 4.6 collective-permute-start.10
  303.3 0.3 collective-permute-start.9
  303.6 3.0 add_convert_fusion.1.refs_11_
  306.6 27.6 %collective-permute-done.13.refs_9_ = bf16[1024,768]{1,0:T(8,128)(2,1)} collective-permute-done((bf16[1024,768]{1,0:T(8,128)(2,1)}, bf16[1024,768]{1,0:T(8,128)(2,1)}, u32[]{:S(2)}, u32[]{:S(2)}) %collective-permute-start.13) | collective-permute-done | bytes 1572896 | tf_op jit(solution)/shard_map/ppermute | solution.py:361
  334.3 33.0 %collective-permute-done.14.refs_10_ = bf16[1024,768]{1,0:T(8,128)(2,1)} collective-permute-done((bf16[1024,768]{1,0:T(8,128)(2,1)}, bf16[1024,768]{1,0:T(8,128)(2,1)}, u32[]{:S(2)}, u32[]{:S(2)}) %collective-permute-start.14) | collective-permute-done | bytes 1572896 | tf_op jit(solution)/shard_map/ppermute | solution.py:361
  367.3 5.0 %collective-permute-done.9.refs_7_ = bf16[1024,768]{1,0:T(8,128)(2,1)} collective-permute-done((bf16[1024,768]{1,0:T(8,128)(2,1)}, bf16[1024,768]{1,0:T(8,128)(2,1)}, u32[]{:S(2)}, u32[]{:S(2)}) %collective-permute-start.9) | collective-permute-done | bytes 1572896 | tf_op jit(solution)/shard_map/ppermute | solution.py:361
  372.3 48.5 %moe_phase.9 = (f32[1024,768]{1,0:T(8,128)}, bf16[1024,768]{1,0:T(8,128)(2,1)}) custom-call(f32[2,8,1024]{2,1,0:T(8,128)} %subtract_select_fusion.3.route_ref, bf16[1024,768]{1,0:T(8,128)(2,1)} %refs_0_.3, bf16[1024,768]{1,0:T(8,128)(2,1)} %collective-permute-done.1.refs_1_, bf16[8,768,2688]{2,1,0:T(8,128)(2,1)} %refs_2_.9, bf16[8,768,2688]{2,1,0:T(8,128)(2,1)} %refs_3_.9, ...), custom_call_target="tpu_custom_call" | custom-call | flops 25367150592 | bytes 49545216 | tf_op jit(solution)/shard_map/moe_phase/pallas_call | solution.py:312
  420.8 0.0 collective-permute-start.20
  420.8 3.1 collective-permute-start.21
  423.9 0.5 collective-permute-done.20
  424.4 34.8 %collective-permute-done.21 = bf16[1024,768]{1,0:T(8,128)(2,1)S(1)} collective-permute-done((bf16[1024,768]{1,0:T(8,128)(2,1)}, bf16[1024,768]{1,0:T(8,128)(2,1)S(1)}, u32[]{:S(2)}, u32[]{:S(2)}) %collective-permute-start.21) | collective-permute-done | bytes 1572896 | tf_op jit(solution)/shard_map/ppermute | solution.py:361
  459.2 3.5 add_convert_fusion
  (9 shorter events, 0.0 us)
Async XLA Ops:
  0.0 8.1 %collective-permute-start.1 = (bf16[1024,768]{1,0:T(8,128)(2,1)}, bf16[1024,768]{1,0:T(8,128)(2,1)}, u32[]{:S(2)}, u32[]{:S(2)}) collective-permute-start(bf16[1024,768]{1,0:T(8,128)(2,1)} %refs_0_.3), channel_id=1, source_target_pairs={{0,1},{1,0},{2,3},{3,2},{4,5},{5,4},{6,7},{7,6}} | collective-permute-start | bytes 4718600 | tf_op jit(solution)/shard_map/ppermute | solution.py:361
  2.3 5.1 %collective-permute-start = (f32[8,1024]{1,0:T(8,128)S(1)}, f32[8,1024]{1,0:T(8,128)S(1)}, u32[]{:S(2)}, u32[]{:S(2)}) collective-permute-start(f32[8,1024]{1,0:T(8,128)S(1)} %get-tuple-element.40), channel_id=1, source_target_pairs={{0,1},{1,0},{2,3},{3,2},{4,5},{5,4},{6,7},{7,6}} | collective-permute-start | bytes 98312 | tf_op jit(solution)/shard_map/ppermute | solution.py:361
  2.3 46.3 %collective-permute-start.2 = (f32[8,1024]{1,0:T(8,128)S(1)}, f32[8,1024]{1,0:T(8,128)}, u32[]{:S(2)}, u32[]{:S(2)}) collective-permute-start(f32[8,1024]{1,0:T(8,128)S(1)} %get-tuple-element.40), channel_id=1, source_target_pairs={{0,2},{1,3},{2,0},{3,1},{4,6},{5,7},{6,4},{7,5}} | collective-permute-start | bytes 98312 | tf_op jit(solution)/shard_map/ppermute | solution.py:361
  5.3 43.3 %collective-permute-start.3 = (f32[8,1024]{1,0:T(8,128)S(1)}, f32[8,1024]{1,0:T(8,128)}, u32[]{:S(2)}, u32[]{:S(2)}) collective-permute-start(f32[8,1024]{1,0:T(8,128)S(1)} %get-tuple-element.40), channel_id=1, source_target_pairs={{0,4},{1,5},{2,6},{3,7},{4,0},{5,1},{6,2},{7,3}} | collective-permute-start | bytes 98312 | tf_op jit(solution)/shard_map/ppermute | solution.py:361
  6.8 41.8 %collective-permute-start.4 = (bf16[1024,768]{1,0:T(8,128)(2,1)}, bf16[1024,768]{1,0:T(8,128)(2,1)}, u32[]{:S(2)}, u32[]{:S(2)}) collective-permute-start(bf16[1024,768]{1,0:T(8,128)(2,1)} %refs_0_.3), channel_id=1, source_target_pairs={{0,2},{1,3},{2,0},{3,1},{4,6},{5,7},{6,4},{7,5}} | collective-permute-start | bytes 4718600 | tf_op jit(solution)/shard_map/ppermute | solution.py:361
  7.4 41.3 %collective-permute-start.5 = (bf16[1024,768]{1,0:T(8,128)(2,1)}, bf16[1024,768]{1,0:T(8,128)(2,1)}, u32[]{:S(2)}, u32[]{:S(2)}) collective-permute-start(bf16[1024,768]{1,0:T(8,128)(2,1)} %refs_0_.3), channel_id=1, source_target_pairs={{0,4},{1,5},{2,6},{3,7},{4,0},{5,1},{6,2},{7,3}} | collective-permute-start | bytes 4718600 | tf_op jit(solution)/shard_map/ppermute | solution.py:361
  48.6 8.5 %collective-permute-start.8 = (bf16[1024,768]{1,0:T(8,128)(2,1)}, bf16[1024,768]{1,0:T(8,128)(2,1)}, u32[]{:S(2)}, u32[]{:S(2)}) collective-permute-start(bf16[1024,768]{1,0:T(8,128)(2,1)} %collective-permute-done.4.refs_0_), channel_id=1, source_target_pairs={{0,1},{1,0},{2,3},{3,2},{4,5},{5,4},{6,7},{7,6}} | collective-permute-start | bytes 4718600 | tf_op jit(solution)/shard_map/ppermute | solution.py:361
  48.7 6.8 %collective-permute-start.7 = (f32[8,1024]{1,0:T(8,128)}, f32[8,1024]{1,0:T(8,128)S(1)}, u32[]{:S(2)}, u32[]{:S(2)}) collective-permute-start(f32[8,1024]{1,0:T(8,128)} %collective-permute-done.2), channel_id=1, source_target_pairs={{0,1},{1,0},{2,3},{3,2},{4,5},{5,4},{6,7},{7,6}} | collective-permute-start | bytes 98312 | tf_op jit(solution)/shard_map/ppermute | solution.py:361
  49.2 6.5 %collective-permute-start.11 = (f32[8,1024]{1,0:T(8,128)}, f32[8,1024]{1,0:T(8,128)S(1)}, u32[]{:S(2)}, u32[]{:S(2)}) collective-permute-start(f32[8,1024]{1,0:T(8,128)} %collective-permute-done.3), channel_id=1, source_target_pairs={{0,1},{1,0},{2,3},{3,2},{4,5},{5,4},{6,7},{7,6}} | collective-permute-start | bytes 98312 | tf_op jit(solution)/shard_map/ppermute | solution.py:361
  49.2 86.6 %collective-permute-start.16 = (bf16[1024,768]{1,0:T(8,128)(2,1)}, bf16[1024,768]{1,0:T(8,128)(2,1)}, u32[]{:S(2)}, u32[]{:S(2)}) collective-permute-start(bf16[1024,768]{1,0:T(8,128)(2,1)} %collective-permute-done.4.refs_0_), channel_id=1, source_target_pairs={{0,4},{1,5},{2,6},{3,7},{4,0},{5,1},{6,2},{7,3}} | collective-permute-start | bytes 4718600 | tf_op jit(solution)/shard_map/ppermute | solution.py:361
  55.4 80.3 %collective-permute-start.15 = (f32[8,1024]{1,0:T(8,128)}, f32[8,1024]{1,0:T(8,128)S(1)}, u32[]{:S(2)}, u32[]{:S(2)}) collective-permute-start(f32[8,1024]{1,0:T(8,128)} %collective-permute-done.2), channel_id=1, source_target_pairs={{0,4},{1,5},{2,6},{3,7},{4,0},{5,1},{6,2},{7,3}} | collective-permute-start | bytes 98312 | tf_op jit(solution)/shard_map/ppermute | solution.py:361
  55.4 80.9 %collective-permute-start.12 = (bf16[1024,768]{1,0:T(8,128)(2,1)}, bf16[1024,768]{1,0:T(8,128)(2,1)}, u32[]{:S(2)}, u32[]{:S(2)}) collective-permute-start(bf16[1024,768]{1,0:T(8,128)(2,1)} %collective-permute-done.5.refs_0_), channel_id=1, source_target_pairs={{0,1},{1,0},{2,3},{3,2},{4,5},{5,4},{6,7},{7,6}} | collective-permute-start | bytes 4718600 | tf_op jit(solution)/shard_map/ppermute | solution.py:361
  135.8 74.8 %collective-permute-start.18 = (bf16[1024,768]{1,0:T(8,128)(2,1)}, bf16[1024,768]{1,0:T(8,128)(2,1)}, u32[]{:S(2)}, u32[]{:S(2)}) collective-permute-start(bf16[1024,768]{1,0:T(8,128)(2,1)} %collective-permute-done.16.refs_0_), channel_id=1, source_target_pairs={{0,1},{1,0},{2,3},{3,2},{4,5},{5,4},{6,7},{7,6}} | collective-permute-start | bytes 4718600 | tf_op jit(solution)/shard_map/ppermute | solution.py:361
  136.1 73.0 %collective-permute-start.17 = (f32[8,1024]{1,0:T(8,128)S(1)}, f32[8,1024]{1,0:T(8,128)}, u32[]{:S(2)}, u32[]{:S(2)}) collective-permute-start(f32[8,1024]{1,0:T(8,128)S(1)} %collective-permute-done.15), channel_id=1, source_target_pairs={{0,1},{1,0},{2,3},{3,2},{4,5},{5,4},{6,7},{7,6}} | collective-permute-start | bytes 98312 | tf_op jit(solution)/shard_map/ppermute | solution.py:361
  289.0 14.3 %collective-permute-start.19 = (bf16[1024,768]{1,0:T(8,128)(2,1)}, bf16[1024,768]{1,0:T(8,128)(2,1)S(1)}, u32[]{:S(2)}, u32[]{:S(2)}) collective-permute-start(bf16[1024,768]{1,0:T(8,128)(2,1)} %get-tuple-element.36), channel_id=1, source_target_pairs={{0,1},{1,0},{2,3},{3,2},{4,5},{5,4},{6,7},{7,6}} | collective-permute-start | bytes 4718600 | tf_op jit(solution)/shard_map/ppermute | solution.py:361
  289.4 17.3 %collective-permute-start.6 = (bf16[1024,768]{1,0:T(8,128)(2,1)}, bf16[1024,768]{1,0:T(8,128)(2,1)}, u32[]{:S(2)}, u32[]{:S(2)}) collective-permute-start(bf16[1024,768]{1,0:T(8,128)(2,1)} %get-tuple-element.24), channel_id=1, source_target_pairs={{0,1},{1,0},{2,3},{3,2},{4,5},{5,4},{6,7},{7,6}} | collective-permute-start | bytes 4718600 | tf_op jit(solution)/shard_map/ppermute | solution.py:361
  289.6 44.7 %collective-permute-start.13 = (bf16[1024,768]{1,0:T(8,128)(2,1)}, bf16[1024,768]{1,0:T(8,128)(2,1)}, u32[]{:S(2)}, u32[]{:S(2)}) collective-permute-start(bf16[1024,768]{1,0:T(8,128)(2,1)} %get-tuple-element.31.refs_5_), channel_id=1, source_target_pairs={{0,4},{1,5},{2,6},{3,7},{4,0},{5,1},{6,2},{7,3}} | collective-permute-start | bytes 4718600 | tf_op jit(solution)/shard_map/ppermute | solution.py:361
  298.7 68.6 %collective-permute-start.14 = (bf16[1024,768]{1,0:T(8,128)(2,1)}, bf16[1024,768]{1,0:T(8,128)(2,1)}, u32[]{:S(2)}, u32[]{:S(2)}) collective-permute-start(bf16[1024,768]{1,0:T(8,128)(2,1)} %get-tuple-element.32), channel_id=1, source_target_pairs={{0,5},{1,4},{2,7},{3,6},{4,1},{5,0},{6,3},{7,2}} | collective-permute-start | bytes 4718600 | tf_op jit(solution)/shard_map/ppermute | solution.py:361
  298.7 68.6 %collective-permute-start.10 = (bf16[1024,768]{1,0:T(8,128)(2,1)}, bf16[1024,768]{1,0:T(8,128)(2,1)}, u32[]{:S(2)}, u32[]{:S(2)}) collective-permute-start(bf16[1024,768]{1,0:T(8,128)(2,1)} %get-tuple-element.28), channel_id=1, source_target_pairs={{0,3},{1,2},{2,1},{3,0},{4,7},{5,6},{6,5},{7,4}} | collective-permute-start | bytes 4718600 | tf_op jit(solution)/shard_map/ppermute | solution.py:361
  303.3 69.0 %collective-permute-start.9 = (bf16[1024,768]{1,0:T(8,128)(2,1)}, bf16[1024,768]{1,0:T(8,128)(2,1)}, u32[]{:S(2)}, u32[]{:S(2)}) collective-permute-start(bf16[1024,768]{1,0:T(8,128)(2,1)} %get-tuple-element.27.refs_5_), channel_id=1, source_target_pairs={{0,2},{1,3},{2,0},{3,1},{4,6},{5,7},{6,4},{7,5}} | collective-permute-start | bytes 4718600 | tf_op jit(solution)/shard_map/ppermute | solution.py:361
  420.8 3.6 collective-permute-start.20
  420.8 38.4 %collective-permute-start.21 = (bf16[1024,768]{1,0:T(8,128)(2,1)}, bf16[1024,768]{1,0:T(8,128)(2,1)S(1)}, u32[]{:S(2)}, u32[]{:S(2)}) collective-permute-start(bf16[1024,768]{1,0:T(8,128)(2,1)} %add_convert_fusion.1.refs_11_), channel_id=1, source_target_pairs={{0,6},{1,7},{2,4},{3,5},{4,2},{5,3},{6,0},{7,1}} | collective-permute-start | bytes 4718600 | tf_op jit(solution)/shard_map/ppermute | solution.py:361

commit v2 on v1

--- a/solution.py
+++ b/solution.py
@@ -91,8 +91,14 @@
         return 0
 
     lax.fori_loop(0, sources, number, 0)
-    rows_ref[...] = jnp.zeros_like(rows_ref)
-    row_gate[...] = jnp.zeros_like(row_gate)
+
+    def clear(i, _):
+        where = pl.ds(pl.multiple_of(lax.rem(i, experts) * stride, 16), stride)
+        rows_ref[i // experts, where, :] = jnp.zeros((stride, d_model), jnp.bfloat16)
+        row_gate[i // experts, where, :] = jnp.zeros((stride, 1), jnp.float32)
+        return 0
+
+    lax.fori_loop(0, sources * experts, clear, 0)
     for copy in tok_copies:
         copy.wait()
     for copy in weight_copies(0, 0):
@@ -219,57 +225,48 @@
             y_ref[e * WINDOW:(e + 1) * WINDOW, :] = rows_ref[s, pl.ds(pl.multiple_of(e * stride + at, 16), WINDOW), :]
         return jnp.concatenate(puts, axis=1)
 
-    def combine(i, put, y_ref):
+    def combine(half, put, y_ref):
+        acc_ref[half] = jnp.dot(put, y_ref[...], preferred_element_type=jnp.float32)
+
+    def finish(half, j):
+        i = 2 * j + half
         s, b = i // blocks, lax.rem(i, blocks)
         span = pl.ds(pl.multiple_of(b * BLOCK, BLOCK), BLOCK)
-        total = jnp.dot(put, y_ref[...], preferred_element_type=jnp.float32)
-        tok_ref[s, span, :] = total.astype(jnp.bfloat16)
-        if adds:
-            acc_ref[...] = total
-
-    def finish(i):
-        s, b = i // blocks, lax.rem(i, blocks)
-        span = pl.ds(pl.multiple_of(b * BLOCK, BLOCK), BLOCK)
-        local = lax.broadcasted_iota(jnp.int32, (BLOCK, WINDOW), 1)
-        extra = extra_windows(s, b)
-
-        @pl.when(extra > 0)
-        def _():
-            acc_ref[...] = jnp.zeros_like(acc_ref)
-
-            def every(i, _):
-                k, e = i // experts, lax.rem(i, experts)
-                _, _, at = bounds(s, b, e)
-                at = at + k * WINDOW
-
-                @pl.when(at < jnp.minimum(base_ref[s, b + 1, e], cap))
-                def _():
-                    col = lax.broadcasted_iota(jnp.int32, (BLOCK, experts), 1)
-                    mine = jnp.sum(jnp.where(col == e, slot_sub[s, span, :], 0.0), axis=1, keepdims=True)
-                    put = ((local + at).astype(jnp.float32) == mine).astype(jnp.bfloat16)
-                    y = rows_ref[s, pl.ds(pl.multiple_of(e * stride + at, 16), WINDOW), :]
-                    acc_ref[...] += jnp.dot(put, y, preferred_element_type=jnp.float32)
-
-                return 0
-
-            lax.fori_loop(0, (extra + 1) * experts, every, 0)
-            tok_ref[s, span, :] = acc_ref[...].astype(jnp.bfloat16)
+
+        def more(j, _):
+            k, e = j // experts + 1, lax.rem(j, experts)
+            _, end, at = bounds(s, b, e)
+            at = at + k * WINDOW
+
+            @pl.when(at < end)
+            def _():
+                col = lax.broadcasted_iota(jnp.int32, (BLOCK, experts), 1)
+                mine = jnp.sum(jnp.where(col == e, slot_sub[s, span, :], 0.0), axis=1, keepdims=True)
+                slots = (lax.broadcasted_iota(jnp.int32, (BLOCK, WINDOW), 1) + at).astype(jnp.float32)
+                y = rows_ref[s, pl.ds(pl.multiple_of(e * stride + at, 16), WINDOW), :]
+                acc_ref[half] += jnp.dot((slots == mine).astype(jnp.bfloat16), y, preferred_element_type=jnp.float32)
+
+            return 0
+
+        lax.fori_loop(0, extra_windows(s, b) * experts, more, 0)
 
         if adds:
 
             @pl.when(s == 0)
             def _():
-                rows = acc_ref[...]
+                total = acc_ref[half]
                 for k in range(adds):
-                    rows += add_ref[k, span, :].astype(jnp.float32)
-                sum_ref[span, :] = rows
+                    total += add_ref[k, span, :].astype(jnp.float32)
+                sum_ref[span, :] = total
                 pltpu.make_async_copy(sum_ref.at[span, :], out_hbm[0].at[span, :], out_sem).start()
 
+        tok_ref[s, span, :] = acc_ref[half].astype(jnp.bfloat16)
         for t in range(1 if adds else 0, sources):
 
             @pl.when(s == t)
             def _():
                 pltpu.make_async_copy(tok_ref.at[t, span, :], out_hbm[t].at[span, :], out_sem).start()
+        return j
 
     if adds:
         for copy in add_copies:
@@ -278,13 +275,9 @@
     def pair(j, _):
         put_a = gather_rows(2 * j, yblk_ref)
         put_b = gather_rows(2 * j + 1, yblk2_ref)
-        combine(2 * j, put_a, yblk_ref)
-        if adds:
-            finish(2 * j)
-        combine(2 * j + 1, put_b, yblk2_ref)
-        if not adds:
-            finish(2 * j)
-        finish(2 * j + 1)
+        combine(0, put_a, yblk_ref)
+        combine(1, put_b, yblk2_ref)
+        lax.fori_loop(0, 2, finish, j)
         return 0
 
     lax.fori_loop(0, sources * blocks // 2, pair, 0)
@@ -326,7 +319,7 @@
             pltpu.VMEM((experts * WINDOW, BLOCK), jnp.bfloat16),
             pltpu.VMEM((experts * WINDOW, d_model), jnp.bfloat16),
             pltpu.VMEM((experts * WINDOW, d_model), jnp.bfloat16),
-            pltpu.VMEM((BLOCK, d_model), jnp.float32),
+            pltpu.VMEM((2, BLOCK, d_model), jnp.float32),
             pltpu.VMEM((sources, experts, tok_dev), jnp.float32),
             pltpu.VMEM((sources, experts, tok_dev), jnp.float32),
             pltpu.VMEM((sources, tok_dev, experts), jnp.float32),

time: 471 us -> 458 us (0.972)
  starting transfers between devices: 31.1 us -> 24.3 us
  Pallas kernels: 319 us -> 314 us
    ppermute x22, starting transfers between devices: 31.1 us -> 24.3 us  [shift(): lax.ppermute(arr, axes, [(rank_of(*r), rank_of(r[0], r[1] ^ flip_ep, r[2]...]
  transfers between devices with their start and end apart: 22 -> 22, of which waited for: 5 -> 5; matrix products, arithmetic and copies ran while one was open for 2% -> 2% of each run, Pallas kernels for 41% -> 42%
where the time goes in v2:
time: 458 us; the launch traced here: 452 us
  Pallas kernels  314 us (69%)
  waiting for transfers between devices  101 us (22%)
  starting transfers between devices  24.3 us (5%)
  other arithmetic  11.6 us (3%)
    pallas_call x5, Pallas kernels, phase(): pl.pallas_call(functools.partial(phase_kernel, cap, small, first, experts...  314 us
    ppermute x22, waiting for transfers between devices, shift(): lax.ppermute(arr, axes, [(rank_of(*r), rank_of(r[0], r[1] ^ flip_ep, r[2]...  101 us
    ppermute x22, starting transfers between devices, shift(): lax.ppermute(arr, axes, [(rank_of(*r), rank_of(r[0], r[1] ^ flip_ep, r[2]...  24.3 us
  transfers between devices with their start and end apart: 22, of which 5 were waited for; matrix products, arithmetic and copies ran while one was open for 2% of the time, Pallas kernels for 42%

profile of v2, /device:TPU:0, one launch (start us, length us, event | category | flops | bytes accessed | tf_op | source)
XLA Modules:
  0.0 451.6 jit_solution(4139843314420844396)
XLA Ops:
  0.0 0.8 collective-permute-start.1
  0.8 0.7 convert_bitcast_fusion
  1.6 0.7 fusion
  2.3 0.0 collective-permute-start
  2.3 3.0 collective-permute-start.2
  5.3 1.5 collective-permute-start.3
  6.8 0.5 collective-permute-start.4
  7.4 0.0 collective-permute-done
  7.4 0.0 collective-permute-start.5
  7.4 0.7 subtract_select_fusion.3.route_ref
  8.1 0.0 collective-permute-done.1.refs_1_
  8.1 41.0 %moe_phase.5 = (bf16[1024,768]{1,0:T(8,128)(2,1)}, bf16[1024,768]{1,0:T(8,128)(2,1)}) custom-call(f32[2,8,1024]{2,1,0:T(8,128)} %subtract_select_fusion.3.route_ref, bf16[1024,768]{1,0:T(8,128)(2,1)} %refs_0_.3, bf16[1024,768]{1,0:T(8,128)(2,1)} %collective-permute-done.1.refs_1_, bf16[8,768,2688]{2,1,0:T(8,128)(2,1)} %refs_2_.9, ...), custom_call_target="tpu_custom_call" | custom-call | flops 25367150592 | bytes 49545216 | tf_op jit(solution)/shard_map/moe_phase/pallas_call | solution.py:305
  49.1 0.0 collective-permute-done.2
  49.1 0.0 collective-permute-done.5.refs_0_
  49.1 0.0 collective-permute-start.8
  49.2 0.5 collective-permute-start.7
  49.7 0.0 collective-permute-start.11
  49.7 4.8 %collective-permute-start.16 = (bf16[1024,768]{1,0:T(8,128)(2,1)}, bf16[1024,768]{1,0:T(8,128)(2,1)}, u32[]{:S(2)}, u32[]{:S(2)}) collective-permute-start(bf16[1024,768]{1,0:T(8,128)(2,1)} %collective-permute-done.4.refs_0_), channel_id=1, source_target_pairs={{0,4},{1,5},{2,6},{3,7},{4,0},{5,1},{6,2},{7,3}} | collective-permute-start | bytes 4718600 | tf_op jit(solution)/shard_map/ppermute | solution.py:354
  54.5 0.0 collective-permute-start.15
  54.5 0.0 collective-permute-done.7
  54.5 0.2 collective-permute-start.12
  54.7 0.0 collective-permute-done.11
  54.7 1.5 subtract_select_fusion.1
  56.2 76.8 %moe_phase.6 = (bf16[1024,768]{1,0:T(8,128)(2,1)}, bf16[1024,768]{1,0:T(8,128)(2,1)}) custom-call(f32[2,8,1024]{2,1,0:T(8,128)} %get-tuple-element.42.route_ref, bf16[1024,768]{1,0:T(8,128)(2,1)} %collective-permute-done.4.refs_0_, bf16[1024,768]{1,0:T(8,128)(2,1)} %collective-permute-done.8.refs_1_, bf16[8,768,2688]{2,1,0:T(8,128)(2,1)} %refs_2_.9, ...), custom_call_target="tpu_custom_call" | custom-call | flops 50734301184 | bytes 99090432 | tf_op jit(solution)/shard_map/moe_phase/pallas_call | solution.py:305
  133.0 0.4 collective-permute-start.18
  133.3 0.2 collective-permute-start.17
  133.5 0.0 collective-permute-done.12.refs_1_
  133.5 73.1 %moe_phase.7 = (bf16[1024,768]{1,0:T(8,128)(2,1)}, bf16[1024,768]{1,0:T(8,128)(2,1)}) custom-call(f32[2,8,1024]{2,1,0:T(8,128)} %get-tuple-element.41.route_ref, bf16[1024,768]{1,0:T(8,128)(2,1)} %collective-permute-done.5.refs_0_, bf16[1024,768]{1,0:T(8,128)(2,1)} %collective-permute-done.12.refs_1_, bf16[8,768,2688]{2,1,0:T(8,128)(2,1)} %refs_2_.9, ...), custom_call_target="tpu_custom_call" | custom-call | flops 50734301184 | bytes 99090432 | tf_op jit(solution)/shard_map/moe_phase/pallas_call | solution.py:305
  206.7 1.5 subtract_select_fusion.route_ref
  208.1 0.0 collective-permute-done.18.refs_1_
  208.1 76.2 %moe_phase.8 = (bf16[1024,768]{1,0:T(8,128)(2,1)}, bf16[1024,768]{1,0:T(8,128)(2,1)}) custom-call(f32[2,8,1024]{2,1,0:T(8,128)} %subtract_select_fusion.route_ref, bf16[1024,768]{1,0:T(8,128)(2,1)} %collective-permute-done.16.refs_0_, bf16[1024,768]{1,0:T(8,128)(2,1)} %collective-permute-done.18.refs_1_, bf16[8,768,2688]{2,1,0:T(8,128)(2,1)} %refs_2_.9, ...), custom_call_target="tpu_custom_call" | custom-call | flops 50734301184 | bytes 99090432 | tf_op jit(solution)/shard_map/moe_phase/pallas_call | solution.py:305
  284.4 0.4 collective-permute-start.19
  284.7 0.2 collective-permute-start.6
  284.9 6.4 %collective-permute-start.13 = (bf16[1024,768]{1,0:T(8,128)(2,1)}, bf16[1024,768]{1,0:T(8,128)(2,1)}, u32[]{:S(2)}, u32[]{:S(2)}) collective-permute-start(bf16[1024,768]{1,0:T(8,128)(2,1)} %get-tuple-element.31.refs_5_), channel_id=1, source_target_pairs={{0,4},{1,5},{2,6},{3,7},{4,0},{5,1},{6,2},{7,3}} | collective-permute-start | bytes 4718600 | tf_op jit(solution)/shard_map/ppermute | solution.py:354
  291.3 1.9 collective-permute-start.10
  293.2 0.0 collective-permute-done.19
  293.2 0.3 collective-permute-start.9
  293.5 3.0 add_convert_fusion.1.refs_11_
  296.5 0.0 collective-permute-done.6.refs_6_
  296.5 30.4 %collective-permute-done.13.refs_9_ = bf16[1024,768]{1,0:T(8,128)(2,1)} collective-permute-done((bf16[1024,768]{1,0:T(8,128)(2,1)}, bf16[1024,768]{1,0:T(8,128)(2,1)}, u32[]{:S(2)}, u32[]{:S(2)}) %collective-permute-start.13) | collective-permute-done | bytes 1572896 | tf_op jit(solution)/shard_map/ppermute | solution.py:354
  326.9 33.1 %collective-permute-done.14.refs_10_ = bf16[1024,768]{1,0:T(8,128)(2,1)} collective-permute-done((bf16[1024,768]{1,0:T(8,128)(2,1)}, bf16[1024,768]{1,0:T(8,128)(2,1)}, u32[]{:S(2)}, u32[]{:S(2)}) %collective-permute-start.14) | collective-permute-done | bytes 1572896 | tf_op jit(solution)/shard_map/ppermute | solution.py:354
  360.0 2.2 collective-permute-done.9.refs_7_
  362.2 47.3 %moe_phase.9 = (f32[1024,768]{1,0:T(8,128)}, bf16[1024,768]{1,0:T(8,128)(2,1)}) custom-call(f32[2,8,1024]{2,1,0:T(8,128)} %subtract_select_fusion.3.route_ref, bf16[1024,768]{1,0:T(8,128)(2,1)} %refs_0_.3, bf16[1024,768]{1,0:T(8,128)(2,1)} %collective-permute-done.1.refs_1_, bf16[8,768,2688]{2,1,0:T(8,128)(2,1)} %refs_2_.9, bf16[8,768,2688]{2,1,0:T(8,128)(2,1)} %refs_3_.9, ...), custom_call_target="tpu_custom_call" | custom-call | flops 25367150592 | bytes 49545216 | tf_op jit(solution)/shard_map/moe_phase/pallas_call | solution.py:305
  409.5 0.0 collective-permute-start.20
  409.5 3.2 collective-permute-start.21
  412.7 0.4 collective-permute-done.20
  413.1 34.8 %collective-permute-done.21 = bf16[1024,768]{1,0:T(8,128)(2,1)S(1)} collective-permute-done((bf16[1024,768]{1,0:T(8,128)(2,1)}, bf16[1024,768]{1,0:T(8,128)(2,1)S(1)}, u32[]{:S(2)}, u32[]{:S(2)}) %collective-permute-start.21) | collective-permute-done | bytes 1572896 | tf_op jit(solution)/shard_map/ppermute | solution.py:354
  447.9 3.5 add_convert_fusion
  (9 shorter events, 0.0 us)
Async XLA Ops:
  0.0 8.1 %collective-permute-start.1 = (bf16[1024,768]{1,0:T(8,128)(2,1)}, bf16[1024,768]{1,0:T(8,128)(2,1)}, u32[]{:S(2)}, u32[]{:S(2)}) collective-permute-start(bf16[1024,768]{1,0:T(8,128)(2,1)} %refs_0_.3), channel_id=1, source_target_pairs={{0,1},{1,0},{2,3},{3,2},{4,5},{5,4},{6,7},{7,6}} | collective-permute-start | bytes 4718600 | tf_op jit(solution)/shard_map/ppermute | solution.py:354
  2.3 5.1 %collective-permute-start = (f32[8,1024]{1,0:T(8,128)S(1)}, f32[8,1024]{1,0:T(8,128)S(1)}, u32[]{:S(2)}, u32[]{:S(2)}) collective-permute-start(f32[8,1024]{1,0:T(8,128)S(1)} %get-tuple-element.40), channel_id=1, source_target_pairs={{0,1},{1,0},{2,3},{3,2},{4,5},{5,4},{6,7},{7,6}} | collective-permute-start | bytes 98312 | tf_op jit(solution)/shard_map/ppermute | solution.py:354
  2.3 46.8 %collective-permute-start.2 = (f32[8,1024]{1,0:T(8,128)S(1)}, f32[8,1024]{1,0:T(8,128)}, u32[]{:S(2)}, u32[]{:S(2)}) collective-permute-start(f32[8,1024]{1,0:T(8,128)S(1)} %get-tuple-element.40), channel_id=1, source_target_pairs={{0,2},{1,3},{2,0},{3,1},{4,6},{5,7},{6,4},{7,5}} | collective-permute-start | bytes 98312 | tf_op jit(solution)/shard_map/ppermute | solution.py:354
  5.3 43.8 %collective-permute-start.3 = (f32[8,1024]{1,0:T(8,128)S(1)}, f32[8,1024]{1,0:T(8,128)}, u32[]{:S(2)}, u32[]{:S(2)}) collective-permute-start(f32[8,1024]{1,0:T(8,128)S(1)} %get-tuple-element.40), channel_id=1, source_target_pairs={{0,4},{1,5},{2,6},{3,7},{4,0},{5,1},{6,2},{7,3}} | collective-permute-start | bytes 98312 | tf_op jit(solution)/shard_map/ppermute | solution.py:354
  6.8 42.3 %collective-permute-start.4 = (bf16[1024,768]{1,0:T(8,128)(2,1)}, bf16[1024,768]{1,0:T(8,128)(2,1)}, u32[]{:S(2)}, u32[]{:S(2)}) collective-permute-start(bf16[1024,768]{1,0:T(8,128)(2,1)} %refs_0_.3), channel_id=1, source_target_pairs={{0,2},{1,3},{2,0},{3,1},{4,6},{5,7},{6,4},{7,5}} | collective-permute-start | bytes 4718600 | tf_op jit(solution)/shard_map/ppermute | solution.py:354
  7.4 41.8 %collective-permute-start.5 = (bf16[1024,768]{1,0:T(8,128)(2,1)}, bf16[1024,768]{1,0:T(8,128)(2,1)}, u32[]{:S(2)}, u32[]{:S(2)}) collective-permute-start(bf16[1024,768]{1,0:T(8,128)(2,1)} %refs_0_.3), channel_id=1, source_target_pairs={{0,4},{1,5},{2,6},{3,7},{4,0},{5,1},{6,2},{7,3}} | collective-permute-start | bytes 4718600 | tf_op jit(solution)/shard_map/ppermute | solution.py:354
  49.1 7.1 %collective-permute-start.8 = (bf16[1024,768]{1,0:T(8,128)(2,1)}, bf16[1024,768]{1,0:T(8,128)(2,1)}, u32[]{:S(2)}, u32[]{:S(2)}) collective-permute-start(bf16[1024,768]{1,0:T(8,128)(2,1)} %collective-permute-done.4.refs_0_), channel_id=1, source_target_pairs={{0,1},{1,0},{2,3},{3,2},{4,5},{5,4},{6,7},{7,6}} | collective-permute-start | bytes 4718600 | tf_op jit(solution)/shard_map/ppermute | solution.py:354
  49.2 5.3 %collective-permute-start.7 = (f32[8,1024]{1,0:T(8,128)}, f32[8,1024]{1,0:T(8,128)S(1)}, u32[]{:S(2)}, u32[]{:S(2)}) collective-permute-start(f32[8,1024]{1,0:T(8,128)} %collective-permute-done.2), channel_id=1, source_target_pairs={{0,1},{1,0},{2,3},{3,2},{4,5},{5,4},{6,7},{7,6}} | collective-permute-start | bytes 98312 | tf_op jit(solution)/shard_map/ppermute | solution.py:354
  49.7 5.0 %collective-permute-start.11 = (f32[8,1024]{1,0:T(8,128)}, f32[8,1024]{1,0:T(8,128)S(1)}, u32[]{:S(2)}, u32[]{:S(2)}) collective-permute-start(f32[8,1024]{1,0:T(8,128)} %collective-permute-done.3), channel_id=1, source_target_pairs={{0,1},{1,0},{2,3},{3,2},{4,5},{5,4},{6,7},{7,6}} | collective-permute-start | bytes 98312 | tf_op jit(solution)/shard_map/ppermute | solution.py:354
  49.7 83.3 %collective-permute-start.16 = (bf16[1024,768]{1,0:T(8,128)(2,1)}, bf16[1024,768]{1,0:T(8,128)(2,1)}, u32[]{:S(2)}, u32[]{:S(2)}) collective-permute-start(bf16[1024,768]{1,0:T(8,128)(2,1)} %collective-permute-done.4.refs_0_), channel_id=1, source_target_pairs={{0,4},{1,5},{2,6},{3,7},{4,0},{5,1},{6,2},{7,3}} | collective-permute-start | bytes 4718600 | tf_op jit(solution)/shard_map/ppermute | solution.py:354
  54.5 78.5 %collective-permute-start.15 = (f32[8,1024]{1,0:T(8,128)}, f32[8,1024]{1,0:T(8,128)S(1)}, u32[]{:S(2)}, u32[]{:S(2)}) collective-permute-start(f32[8,1024]{1,0:T(8,128)} %collective-permute-done.2), channel_id=1, source_target_pairs={{0,4},{1,5},{2,6},{3,7},{4,0},{5,1},{6,2},{7,3}} | collective-permute-start | bytes 98312 | tf_op jit(solution)/shard_map/ppermute | solution.py:354
  54.5 79.0 %collective-permute-start.12 = (bf16[1024,768]{1,0:T(8,128)(2,1)}, bf16[1024,768]{1,0:T(8,128)(2,1)}, u32[]{:S(2)}, u32[]{:S(2)}) collective-permute-start(bf16[1024,768]{1,0:T(8,128)(2,1)} %collective-permute-done.5.refs_0_), channel_id=1, source_target_pairs={{0,1},{1,0},{2,3},{3,2},{4,5},{5,4},{6,7},{7,6}} | collective-permute-start | bytes 4718600 | tf_op jit(solution)/shard_map/ppermute | solution.py:354
  133.0 75.2 %collective-permute-start.18 = (bf16[1024,768]{1,0:T(8,128)(2,1)}, bf16[1024,768]{1,0:T(8,128)(2,1)}, u32[]{:S(2)}, u32[]{:S(2)}) collective-permute-start(bf16[1024,768]{1,0:T(8,128)(2,1)} %collective-permute-done.16.refs_0_), channel_id=1, source_target_pairs={{0,1},{1,0},{2,3},{3,2},{4,5},{5,4},{6,7},{7,6}} | collective-permute-start | bytes 4718600 | tf_op jit(solution)/shard_map/ppermute | solution.py:354
  133.3 73.3 %collective-permute-start.17 = (f32[8,1024]{1,0:T(8,128)S(1)}, f32[8,1024]{1,0:T(8,128)}, u32[]{:S(2)}, u32[]{:S(2)}) collective-permute-start(f32[8,1024]{1,0:T(8,128)S(1)} %collective-permute-done.15), channel_id=1, source_target_pairs={{0,1},{1,0},{2,3},{3,2},{4,5},{5,4},{6,7},{7,6}} | collective-permute-start | bytes 98312 | tf_op jit(solution)/shard_map/ppermute | solution.py:354
  284.4 8.8 %collective-permute-start.19 = (bf16[1024,768]{1,0:T(8,128)(2,1)}, bf16[1024,768]{1,0:T(8,128)(2,1)S(1)}, u32[]{:S(2)}, u32[]{:S(2)}) collective-permute-start(bf16[1024,768]{1,0:T(8,128)(2,1)} %get-tuple-element.36), channel_id=1, source_target_pairs={{0,1},{1,0},{2,3},{3,2},{4,5},{5,4},{6,7},{7,6}} | collective-permute-start | bytes 4718600 | tf_op jit(solution)/shard_map/ppermute | solution.py:354
  284.7 11.8 %collective-permute-start.6 = (bf16[1024,768]{1,0:T(8,128)(2,1)}, bf16[1024,768]{1,0:T(8,128)(2,1)}, u32[]{:S(2)}, u32[]{:S(2)}) collective-permute-start(bf16[1024,768]{1,0:T(8,128)(2,1)} %get-tuple-element.24), channel_id=1, source_target_pairs={{0,1},{1,0},{2,3},{3,2},{4,5},{5,4},{6,7},{7,6}} | collective-permute-start | bytes 4718600 | tf_op jit(solution)/shard_map/ppermute | solution.py:354
  284.9 42.0 %collective-permute-start.13 = (bf16[1024,768]{1,0:T(8,128)(2,1)}, bf16[1024,768]{1,0:T(8,128)(2,1)}, u32[]{:S(2)}, u32[]{:S(2)}) collective-permute-start(bf16[1024,768]{1,0:T(8,128)(2,1)} %get-tuple-element.31.refs_5_), channel_id=1, source_target_pairs={{0,4},{1,5},{2,6},{3,7},{4,0},{5,1},{6,2},{7,3}} | collective-permute-start | bytes 4718600 | tf_op jit(solution)/shard_map/ppermute | solution.py:354
  291.3 68.6 %collective-permute-start.14 = (bf16[1024,768]{1,0:T(8,128)(2,1)}, bf16[1024,768]{1,0:T(8,128)(2,1)}, u32[]{:S(2)}, u32[]{:S(2)}) collective-permute-start(bf16[1024,768]{1,0:T(8,128)(2,1)} %get-tuple-element.32), channel_id=1, source_target_pairs={{0,5},{1,4},{2,7},{3,6},{4,1},{5,0},{6,3},{7,2}} | collective-permute-start | bytes 4718600 | tf_op jit(solution)/shard_map/ppermute | solution.py:354
  291.3 68.6 %collective-permute-start.10 = (bf16[1024,768]{1,0:T(8,128)(2,1)}, bf16[1024,768]{1,0:T(8,128)(2,1)}, u32[]{:S(2)}, u32[]{:S(2)}) collective-permute-start(bf16[1024,768]{1,0:T(8,128)(2,1)} %get-tuple-element.28), channel_id=1, source_target_pairs={{0,3},{1,2},{2,1},{3,0},{4,7},{5,6},{6,5},{7,4}} | collective-permute-start | bytes 4718600 | tf_op jit(solution)/shard_map/ppermute | solution.py:354
  293.2 69.0 %collective-permute-start.9 = (bf16[1024,768]{1,0:T(8,128)(2,1)}, bf16[1024,768]{1,0:T(8,128)(2,1)}, u32[]{:S(2)}, u32[]{:S(2)}) collective-permute-start(bf16[1024,768]{1,0:T(8,128)(2,1)} %get-tuple-element.27.refs_5_), channel_id=1, source_target_pairs={{0,2},{1,3},{2,0},{3,1},{4,6},{5,7},{6,4},{7,5}} | collective-permute-start | bytes 4718600 | tf_op jit(solution)/shard_map/ppermute | solution.py:354
  409.5 3.6 collective-permute-start.20
  409.5 38.4 %collective-permute-start.21 = (bf16[1024,768]{1,0:T(8,128)(2,1)}, bf16[1024,768]{1,0:T(8,128)(2,1)S(1)}, u32[]{:S(2)}, u32[]{:S(2)}) collective-permute-start(bf16[1024,768]{1,0:T(8,128)(2,1)} %add_convert_fusion.1.refs_11_), channel_id=1, source_target_pairs={{0,6},{1,7},{2,4},{3,5},{4,2},{5,3},{6,0},{7,1}} | collective-permute-start | bytes 4718600 | tf_op jit(solution)/shard_map/ppermute | solution.py:354

commit v3 on v2

--- a/solution.py
+++ b/solution.py
@@ -15,6 +15,7 @@
 CHUNK = 512
 BLOCK = 256
 PARTS = 3
+GROUP = 8
 WINDOW = 128
 
 
@@ -22,20 +23,22 @@
     return [(lo, min(step, width - lo)) for lo in range(0, width, step)]
 
 
-def phase_kernel(cap, small, first, experts, pieces, adds, waits, route_ref, *refs):
+def phase_kernel(cap, small, first, experts, sources, pieces, adds, waits, rank_ref, *refs):
+    route_hbm, refs = refs[:sources], refs[sources:]
     tok_hbm, refs = refs[:pieces], refs[pieces:]
     wg_hbm, wu_hbm, wd_hbm = refs[:3]
     add_hbm = refs[3:3 + adds]
     refs = refs[3 + adds + waits:]
-    sources, lines, toks = route_ref.shape
     out_hbm = refs[:sources]
     (wg_buf, wu_buf, wx_buf, wd_buf, tok_ref, rows_ref, pick_ref, yblk_ref, yblk2_ref, acc_ref, slot_lane, gate_lane, slot_sub, row_gate, h_ref,
-     base_ref, sems, tok_sems, out_sem, *sum_refs) = refs[sources:]
+     base_ref, sems, tok_sems, out_sem, route_ref, route_sems, *sum_refs) = refs[sources:]
+    _, lines, toks = route_ref.shape
     d_model = tok_ref.shape[2]
     top_k = lines // 2
     ff = wg_hbm.shape[2]
     blocks = toks // BLOCK
     stride = cap + WINDOW
+    group_size = min(GROUP, experts)
     main = wg_buf.shape[2]
 
     def weight_copies(e, buf):
@@ -57,11 +60,12 @@
         pltpu.make_async_copy(tok_hbm[p], tok_ref.at[p * size // toks, pl.ds(p * size % toks, size), :], tok_sems.at[p])
         for p in range(pieces)
     ]
-    for copy in tok_copies:
+    route_copies = [pltpu.make_async_copy(route_hbm[s], route_ref.at[s], route_sems.at[s]) for s in range(sources)]
+    for copy in route_copies + tok_copies:
         copy.start()
 
     tri = (lax.broadcasted_iota(jnp.int32, (128, 128), 0) < lax.broadcasted_iota(jnp.int32, (128, 128), 1)).astype(jnp.bfloat16)
-    expert_row = (lax.broadcasted_iota(jnp.int32, (experts, toks), 0) + first).astype(jnp.float32)
+    expert_row = (lax.broadcasted_iota(jnp.int32, (experts, toks), 0) + first + rank_ref[0]).astype(jnp.float32)
 
     def number(s, _):
         hit = jnp.zeros((experts, toks), jnp.float32)
@@ -90,7 +94,11 @@
         slot_sub[s] = jnp.transpose(slot)
         return 0
 
+    for copy in route_copies:
+        copy.wait()
     lax.fori_loop(0, sources, number, 0)
+    for copy in weight_copies(0, 0):
+        copy.start()
 
     def clear(i, _):
         where = pl.ds(pl.multiple_of(lax.rem(i, experts) * stride, 16), stride)
@@ -101,8 +109,6 @@
     lax.fori_loop(0, sources * experts, clear, 0)
     for copy in tok_copies:
         copy.wait()
-    for copy in weight_copies(0, 0):
-        copy.start()
     if adds:
         add_ref, sum_ref, add_sem = sum_refs
         add_copies = [pltpu.make_async_copy(add_hbm[i], add_ref.at[i], add_sem.at[i]) for i in range(adds)]
@@ -135,22 +141,22 @@
         span = pl.ds(pl.multiple_of(b * BLOCK, BLOCK), BLOCK)
         local = lax.broadcasted_iota(jnp.int32, (WINDOW, BLOCK), 0)
 
-        def one_hot(e, at):
-            return (local + at).astype(jnp.float32) == slot_lane[s, e:e + 1, span]
-
-        def gates_of(pick, e):
-            return jnp.sum(jnp.where(pick, gate_lane[s, e:e + 1, span], 0.0), axis=1, keepdims=True)
-
-        gates = []
-        for e in range(experts):
-            _, _, at = bounds(s, b, e)
-            pick = one_hot(e, at)
-            gates.append(gates_of(pick, e))
-            pick_ref[e * WINDOW:(e + 1) * WINDOW, :] = pick.astype(jnp.bfloat16)
-        new = jnp.dot(pick_ref[...], tok_ref[s, span, :], preferred_element_type=jnp.float32)
-        for e in range(experts):
-            begin, _, at = bounds(s, b, e)
-            put_rows(s, e, at, begin, new[e * WINDOW:(e + 1) * WINDOW, :], gates[e])
+        def group(g):
+            gates = []
+            for i in range(group_size):
+                e = g * group_size + i
+                _, _, at = bounds(s, b, e)
+                pick = (local + at).astype(jnp.float32) == slot_lane[s, e:e + 1, span]
+                gates.append(jnp.sum(jnp.where(pick, gate_lane[s, e:e + 1, span], 0.0), axis=1, keepdims=True))
+                pick_ref[i * WINDOW:(i + 1) * WINDOW, :] = pick.astype(jnp.bfloat16)
+            new = jnp.dot(pick_ref[...], tok_ref[s, span, :], preferred_element_type=jnp.float32)
+            for i in range(group_size):
+                e = g * group_size + i
+                begin, _, at = bounds(s, b, e)
+                put_rows(s, e, at, begin, new[i * WINDOW:(i + 1) * WINDOW, :], gates[i])
+
+        for g in range(experts // group_size):
+            group(g)
 
         def more(j, _):
             k, e = j // experts + 1, lax.rem(j, experts)
@@ -286,14 +292,13 @@
         pltpu.make_async_copy(src, out_hbm[s], out_sem).wait()
 
 
-def phase(routes, toks, wg, wu, wd, cap, first=0, experts=None, adds=(), after=()):
-    sources, _, tok_dev = routes.shape
+def phase(rank, routes, toks, wg, wu, wd, cap, first=0, experts=None, adds=(), after=()):
+    sources, (lines, tok_dev) = len(routes), routes[0].shape
     d_model = toks[0].shape[1]
     ff = wg.shape[2]
     main = ff // 256 * 256
     experts = experts or wg.shape[0]
     small = min(cap, 256)
-    vm = pl.BlockSpec(memory_space=pltpu.VMEM)
     hbm = pl.BlockSpec(memory_space=pl.ANY)
     blocks = tok_dev // BLOCK
     height = experts * (cap + WINDOW)
@@ -303,11 +308,11 @@
         pltpu.SemaphoreType.DMA((len(adds),)),
     ] if adds else []
     return pl.pallas_call(
-        functools.partial(phase_kernel, cap, small, first, experts, len(toks), len(adds), len(after)),
+        functools.partial(phase_kernel, cap, small, first, experts, sources, len(toks), len(adds), len(after)),
         out_shape=[
             jax.ShapeDtypeStruct((tok_dev, d_model), jnp.float32 if adds and s == 0 else jnp.bfloat16) for s in range(sources)
         ],
-        in_specs=[vm] + [hbm] * (len(toks) + 3 + len(adds) + len(after)),
+        in_specs=[pl.BlockSpec(memory_space=pltpu.SMEM)] + [hbm] * (sources + len(toks) + 3 + len(adds) + len(after)),
         out_specs=[hbm] * sources,
         scratch_shapes=[
             pltpu.VMEM((2, d_model, main), jnp.bfloat16),
@@ -316,7 +321,7 @@
             pltpu.VMEM((2, ff, d_model), jnp.bfloat16),
             pltpu.VMEM((sources, tok_dev, d_model), jnp.bfloat16),
             pltpu.VMEM((sources, height, d_model), jnp.bfloat16),
-            pltpu.VMEM((experts * WINDOW, BLOCK), jnp.bfloat16),
+            pltpu.VMEM((min(GROUP, experts) * WINDOW, BLOCK), jnp.bfloat16),
             pltpu.VMEM((experts * WINDOW, d_model), jnp.bfloat16),
             pltpu.VMEM((experts * WINDOW, d_model), jnp.bfloat16),
             pltpu.VMEM((2, BLOCK, d_model), jnp.float32),
@@ -329,6 +334,8 @@
             pltpu.SemaphoreType.DMA((2, 3 * PARTS + 2)),
             pltpu.SemaphoreType.DMA((len(toks),)),
             pltpu.SemaphoreType.DMA,
+            pltpu.VMEM((sources, lines, tok_dev), jnp.float32),
+            pltpu.SemaphoreType.DMA((sources,)),
         ] + sum_scratch,
         compiler_params=pltpu.CompilerParams(vmem_limit_bytes=67_000_000),
         cost_estimate=pl.CostEstimate(
@@ -337,7 +344,7 @@
             transcendentals=0,
         ),
         name="moe_phase",
-    )(routes, *toks, wg, wu, wd, *adds, *after)
+    )(rank, *routes, *toks, wg, wu, wd, *adds, *after)
 
 
 def solution(mesh):
@@ -358,14 +365,11 @@
         top_k = expert_ids.shape[1]
         local_experts = w_gate.shape[0]
         capacity = 5 * top_k * tok_dev // (4 * local_experts * ep_size)
-        first = (lax.axis_index("ep") * local_experts).astype(jnp.float32)
+        rank = (lax.axis_index("ep") * local_experts).astype(jnp.int32).reshape(1)
         routes = jnp.concatenate([expert_ids.T.astype(jnp.float32), gates.T], axis=0)
 
         def run(tok_list, route_list, after=(), **part):
-            stacked = jnp.stack(route_list)
-            lines = jnp.arange(2 * top_k)[None, :, None] < top_k
-            stacked = jnp.where(lines, stacked - first, stacked)
-            return phase(stacked, tok_list, w_gate, w_up, w_down, capacity, after=after, **part)
+            return phase(rank, route_list, tok_list, w_gate, w_up, w_down, capacity, after=after, **part)
 
         t_p, r_p = shift(tokens, 0, 1), shift(routes, 0, 1)
         r_x, r_y, t_x, t_y = shift(routes, 0, 2), shift(routes, 1, 0), shift(tokens, 0, 2), shift(tokens, 1, 0)

time: 458 us -> 453 us (0.989)
  transfers between devices with their start and end apart: 22 -> 22, of which waited for: 5 -> 5; matrix products, arithmetic and copies ran while one was open for 2% -> 1% of each run, Pallas kernels for 42% -> 43%
where the time goes in v3:
time: 453 us; the launch traced here: 446 us
  Pallas kernels  312 us (69%)
  waiting for transfers between devices  101 us (22%)
  starting transfers between devices  24.3 us (5%)
  other arithmetic  7.95 us (2%)
    pallas_call x5, Pallas kernels, phase(): pl.pallas_call(functools.partial(phase_kernel, cap, small, first, experts...  312 us
    ppermute x22, waiting for transfers between devices, shift(): lax.ppermute(arr, axes, [(rank_of(*r), rank_of(r[0], r[1] ^ flip_ep, r[2]...  101 us
    ppermute x22, starting transfers between devices, shift(): lax.ppermute(arr, axes, [(rank_of(*r), rank_of(r[0], r[1] ^ flip_ep, r[2]...  24.3 us
  transfers between devices with their start and end apart: 22, of which 5 were waited for; matrix products, arithmetic and copies ran while one was open for 1% of the time, Pallas kernels for 43%

profile of v3, /device:TPU:0, one launch (start us, length us, event | category | flops | bytes accessed | tf_op | source)
XLA Modules:
  0.0 446.4 jit_solution(15047310179010055699)
XLA Ops:
  0.0 0.8 collective-permute-start.1
  0.8 0.7 convert_bitcast_fusion
  1.6 0.7 pad_maximum_fusion.refs_0_
  2.3 0.0 collective-permute-start
  2.3 3.0 collective-permute-start.2
  5.3 1.5 collective-permute-start.3
  6.8 0.5 collective-permute-start.4
  7.4 0.0 collective-permute-done.refs_1_
  7.4 0.6 copy-done.1
  8.0 0.0 collective-permute-start.5
  8.0 0.0 collective-permute-done.1.refs_3_
  8.0 40.4 %moe_phase.5 = (bf16[1024,768]{1,0:T(8,128)(2,1)}, bf16[1024,768]{1,0:T(8,128)(2,1)}) custom-call(s32[1]{0:T(128)} %bitcast.rank_ref, f32[8,1024]{1,0:T(8,128)} %copy-done, f32[8,1024]{1,0:T(8,128)} %copy-done.1, bf16[1024,768]{1,0:T(8,128)(2,1)} %refs_2_.3, bf16[1024,768]{1,0:T(8,128)(2,1)} %collective-permute-done.1.refs_3_, ...), custom_call_target="tpu_custom_call" | custom-call | flops 25367150592 | bytes 49545216 | tf_op jit(solution)/shard_map/moe_phase/pallas_call | solution.py:310
  48.4 0.0 collective-permute-done.2.refs_0_
  48.4 0.0 collective-permute-done.3.refs_0_
  48.4 0.0 collective-permute-done.4.refs_2_
  48.4 0.0 collective-permute-start.8
  48.4 0.5 collective-permute-start.7
  48.9 4.8 %collective-permute-start.16 = (bf16[1024,768]{1,0:T(8,128)(2,1)}, bf16[1024,768]{1,0:T(8,128)(2,1)}, u32[]{:S(2)}, u32[]{:S(2)}) collective-permute-start(bf16[1024,768]{1,0:T(8,128)(2,1)} %collective-permute-done.4.refs_2_), channel_id=1, source_target_pairs={{0,4},{1,5},{2,6},{3,7},{4,0},{5,1},{6,2},{7,3}} | collective-permute-start | bytes 4718600 | tf_op jit(solution)/shard_map/ppermute | solution.py:361
  53.7 0.0 collective-permute-start.15
  53.7 0.0 collective-permute-start.12
  53.7 0.0 collective-permute-done.7.refs_1_
  53.7 0.5 collective-permute-start.11
  54.2 0.0 collective-permute-done.8.refs_3_
  54.2 77.2 %moe_phase.6 = (bf16[1024,768]{1,0:T(8,128)(2,1)}, bf16[1024,768]{1,0:T(8,128)(2,1)}) custom-call(s32[1]{0:T(128)} %bitcast.rank_ref, f32[8,1024]{1,0:T(8,128)} %collective-permute-done.2.refs_0_, f32[8,1024]{1,0:T(8,128)} %collective-permute-done.7.refs_1_, bf16[1024,768]{1,0:T(8,128)(2,1)} %collective-permute-done.4.refs_2_, ...), custom_call_target="tpu_custom_call" | custom-call | flops 50734301184 | bytes 99090432 | tf_op jit(solution)/shard_map/moe_phase/pallas_call | solution.py:310
  131.4 0.0 collective-permute-done.15.refs_0_
  131.4 0.0 collective-permute-done.16.refs_2_
  131.4 0.0 collective-permute-start.18
  131.5 0.5 collective-permute-start.17
  132.0 73.6 %moe_phase.7 = (bf16[1024,768]{1,0:T(8,128)(2,1)}, bf16[1024,768]{1,0:T(8,128)(2,1)}) custom-call(s32[1]{0:T(128)} %bitcast.rank_ref, f32[8,1024]{1,0:T(8,128)} %collective-permute-done.3.refs_0_, f32[8,1024]{1,0:T(8,128)} %collective-permute-done.11.refs_1_, bf16[1024,768]{1,0:T(8,128)(2,1)} %collective-permute-done.5.refs_2_, ...), custom_call_target="tpu_custom_call" | custom-call | flops 50734301184 | bytes 99090432 | tf_op jit(solution)/shard_map/moe_phase/pallas_call | solution.py:310
  205.6 0.0 collective-permute-done.17.refs_1_
  205.6 76.6 %moe_phase.8 = (bf16[1024,768]{1,0:T(8,128)(2,1)}, bf16[1024,768]{1,0:T(8,128)(2,1)}) custom-call(s32[1]{0:T(128)} %bitcast.rank_ref, f32[8,1024]{1,0:T(8,128)} %copy-done.2, f32[8,1024]{1,0:T(8,128)} %collective-permute-done.17.refs_1_, bf16[1024,768]{1,0:T(8,128)(2,1)} %collective-permute-done.16.refs_2_, ...), custom_call_target="tpu_custom_call" | custom-call | flops 50734301184 | bytes 99090432 | tf_op jit(solution)/shard_map/moe_phase/pallas_call | solution.py:310
  282.2 0.1 collective-permute-start.19
  282.3 0.5 collective-permute-start.6
  282.8 6.2 %collective-permute-start.13 = (bf16[1024,768]{1,0:T(8,128)(2,1)}, bf16[1024,768]{1,0:T(8,128)(2,1)}, u32[]{:S(2)}, u32[]{:S(2)}) collective-permute-start(bf16[1024,768]{1,0:T(8,128)(2,1)} %get-tuple-element.31.refs_7_), channel_id=1, source_target_pairs={{0,4},{1,5},{2,6},{3,7},{4,0},{5,1},{6,2},{7,3}} | collective-permute-start | bytes 4718600 | tf_op jit(solution)/shard_map/ppermute | solution.py:361
  289.0 2.1 collective-permute-start.10
  291.1 0.0 collective-permute-done.19
  291.1 0.3 collective-permute-start.9
  291.4 3.0 add_convert_fusion.1.refs_13_
  294.4 0.0 collective-permute-done.6.refs_8_
  294.4 30.1 %collective-permute-done.13.refs_11_ = bf16[1024,768]{1,0:T(8,128)(2,1)} collective-permute-done((bf16[1024,768]{1,0:T(8,128)(2,1)}, bf16[1024,768]{1,0:T(8,128)(2,1)}, u32[]{:S(2)}, u32[]{:S(2)}) %collective-permute-start.13) | collective-permute-done | bytes 1572896 | tf_op jit(solution)/shard_map/ppermute | solution.py:361
  324.5 33.1 %collective-permute-done.14.refs_12_ = bf16[1024,768]{1,0:T(8,128)(2,1)} collective-permute-done((bf16[1024,768]{1,0:T(8,128)(2,1)}, bf16[1024,768]{1,0:T(8,128)(2,1)}, u32[]{:S(2)}, u32[]{:S(2)}) %collective-permute-start.14) | collective-permute-done | bytes 1572896 | tf_op jit(solution)/shard_map/ppermute | solution.py:361
  357.6 2.4 collective-permute-done.9.refs_9_
  360.0 44.5 %moe_phase.9 = (f32[1024,768]{1,0:T(8,128)}, bf16[1024,768]{1,0:T(8,128)(2,1)}) custom-call(s32[1]{0:T(128)} %bitcast.rank_ref, f32[8,1024]{1,0:T(8,128)} %copy-done, f32[8,1024]{1,0:T(8,128)} %copy-done.1, bf16[1024,768]{1,0:T(8,128)(2,1)} %refs_2_.3, bf16[1024,768]{1,0:T(8,128)(2,1)} %collective-permute-done.1.refs_3_, bf16[8,768,2688]{2,1,0:T(8,128)(2,1)} %refs_4_.9, ...), custom_call_target="tpu_custom_call" | custom-call | flops 25367150592 | bytes 49545216 | tf_op jit(solution)/shard_map/moe_phase/pallas_call | solution.py:310
  404.5 0.0 collective-permute-start.20
  404.6 2.9 collective-permute-start.21
  407.5 0.7 collective-permute-done.20
  408.2 34.5 %collective-permute-done.21 = bf16[1024,768]{1,0:T(8,128)(2,1)S(1)} collective-permute-done((bf16[1024,768]{1,0:T(8,128)(2,1)}, bf16[1024,768]{1,0:T(8,128)(2,1)S(1)}, u32[]{:S(2)}, u32[]{:S(2)}) %collective-permute-start.21) | collective-permute-done | bytes 1572896 | tf_op jit(solution)/shard_map/ppermute | solution.py:361
  442.7 3.5 add_convert_fusion
  (11 shorter events, 0.0 us)
Async XLA Ops:
  0.0 8.0 %collective-permute-start.1 = (bf16[1024,768]{1,0:T(8,128)(2,1)}, bf16[1024,768]{1,0:T(8,128)(2,1)}, u32[]{:S(2)}, u32[]{:S(2)}) collective-permute-start(bf16[1024,768]{1,0:T(8,128)(2,1)} %refs_2_.3), channel_id=1, source_target_pairs={{0,1},{1,0},{2,3},{3,2},{4,5},{5,4},{6,7},{7,6}} | collective-permute-start | bytes 4718600 | tf_op jit(solution)/shard_map/ppermute | solution.py:361
  2.3 5.7 %copy-start = (f32[8,1024]{1,0:T(8,128)}, f32[8,1024]{1,0:T(8,128)S(1)}, u32[]{:S(2)}) copy-start(f32[8,1024]{1,0:T(8,128)S(1)} %pad_maximum_fusion.refs_0_) | copy-start | bytes 98308
  2.3 5.1 %collective-permute-start = (f32[8,1024]{1,0:T(8,128)S(1)}, f32[8,1024]{1,0:T(8,128)S(1)}, u32[]{:S(2)}, u32[]{:S(2)}) collective-permute-start(f32[8,1024]{1,0:T(8,128)S(1)} %pad_maximum_fusion.refs_0_), channel_id=1, source_target_pairs={{0,1},{1,0},{2,3},{3,2},{4,5},{5,4},{6,7},{7,6}} | collective-permute-start | bytes 98312 | tf_op jit(solution)/shard_map/ppermute | solution.py:361
  2.3 46.0 %collective-permute-start.2 = (f32[8,1024]{1,0:T(8,128)S(1)}, f32[8,1024]{1,0:T(8,128)}, u32[]{:S(2)}, u32[]{:S(2)}) collective-permute-start(f32[8,1024]{1,0:T(8,128)S(1)} %pad_maximum_fusion.refs_0_), channel_id=1, source_target_pairs={{0,2},{1,3},{2,0},{3,1},{4,6},{5,7},{6,4},{7,5}} | collective-permute-start | bytes 98312 | tf_op jit(solution)/shard_map/ppermute | solution.py:361
  5.3 43.1 %collective-permute-start.3 = (f32[8,1024]{1,0:T(8,128)S(1)}, f32[8,1024]{1,0:T(8,128)}, u32[]{:S(2)}, u32[]{:S(2)}) collective-permute-start(f32[8,1024]{1,0:T(8,128)S(1)} %pad_maximum_fusion.refs_0_), channel_id=1, source_target_pairs={{0,4},{1,5},{2,6},{3,7},{4,0},{5,1},{6,2},{7,3}} | collective-permute-start | bytes 98312 | tf_op jit(solution)/shard_map/ppermute | solution.py:361
  6.8 41.6 %collective-permute-start.4 = (bf16[1024,768]{1,0:T(8,128)(2,1)}, bf16[1024,768]{1,0:T(8,128)(2,1)}, u32[]{:S(2)}, u32[]{:S(2)}) collective-permute-start(bf16[1024,768]{1,0:T(8,128)(2,1)} %refs_2_.3), channel_id=1, source_target_pairs={{0,2},{1,3},{2,0},{3,1},{4,6},{5,7},{6,4},{7,5}} | collective-permute-start | bytes 4718600 | tf_op jit(solution)/shard_map/ppermute | solution.py:361
  7.4 0.6 copy-start.1
  8.0 40.4 %collective-permute-start.5 = (bf16[1024,768]{1,0:T(8,128)(2,1)}, bf16[1024,768]{1,0:T(8,128)(2,1)}, u32[]{:S(2)}, u32[]{:S(2)}) collective-permute-start(bf16[1024,768]{1,0:T(8,128)(2,1)} %refs_2_.3), channel_id=1, source_target_pairs={{0,4},{1,5},{2,6},{3,7},{4,0},{5,1},{6,2},{7,3}} | collective-permute-start | bytes 4718600 | tf_op jit(solution)/shard_map/ppermute | solution.py:361
  48.4 5.8 %collective-permute-start.8 = (bf16[1024,768]{1,0:T(8,128)(2,1)}, bf16[1024,768]{1,0:T(8,128)(2,1)}, u32[]{:S(2)}, u32[]{:S(2)}) collective-permute-start(bf16[1024,768]{1,0:T(8,128)(2,1)} %collective-permute-done.4.refs_2_), channel_id=1, source_target_pairs={{0,1},{1,0},{2,3},{3,2},{4,5},{5,4},{6,7},{7,6}} | collective-permute-start | bytes 4718600 | tf_op jit(solution)/shard_map/ppermute | solution.py:361
  48.4 5.3 %collective-permute-start.7 = (f32[8,1024]{1,0:T(8,128)}, f32[8,1024]{1,0:T(8,128)}, u32[]{:S(2)}, u32[]{:S(2)}) collective-permute-start(f32[8,1024]{1,0:T(8,128)} %collective-permute-done.2.refs_0_), channel_id=1, source_target_pairs={{0,1},{1,0},{2,3},{3,2},{4,5},{5,4},{6,7},{7,6}} | collective-permute-start | bytes 98312 | tf_op jit(solution)/shard_map/ppermute | solution.py:361
  48.9 82.5 %collective-permute-start.16 = (bf16[1024,768]{1,0:T(8,128)(2,1)}, bf16[1024,768]{1,0:T(8,128)(2,1)}, u32[]{:S(2)}, u32[]{:S(2)}) collective-permute-start(bf16[1024,768]{1,0:T(8,128)(2,1)} %collective-permute-done.4.refs_2_), channel_id=1, source_target_pairs={{0,4},{1,5},{2,6},{3,7},{4,0},{5,1},{6,2},{7,3}} | collective-permute-start | bytes 4718600 | tf_op jit(solution)/shard_map/ppermute | solution.py:361
  53.7 77.7 %collective-permute-start.15 = (f32[8,1024]{1,0:T(8,128)}, f32[8,1024]{1,0:T(8,128)S(1)}, u32[]{:S(2)}, u32[]{:S(2)}) collective-permute-start(f32[8,1024]{1,0:T(8,128)} %collective-permute-done.2.refs_0_), channel_id=1, source_target_pairs={{0,4},{1,5},{2,6},{3,7},{4,0},{5,1},{6,2},{7,3}} | collective-permute-start | bytes 98312 | tf_op jit(solution)/shard_map/ppermute | solution.py:361
  53.7 78.3 %collective-permute-start.12 = (bf16[1024,768]{1,0:T(8,128)(2,1)}, bf16[1024,768]{1,0:T(8,128)(2,1)}, u32[]{:S(2)}, u32[]{:S(2)}) collective-permute-start(bf16[1024,768]{1,0:T(8,128)(2,1)} %collective-permute-done.5.refs_2_), channel_id=1, source_target_pairs={{0,1},{1,0},{2,3},{3,2},{4,5},{5,4},{6,7},{7,6}} | collective-permute-start | bytes 4718600 | tf_op jit(solution)/shard_map/ppermute | solution.py:361
  53.7 78.3 %collective-permute-start.11 = (f32[8,1024]{1,0:T(8,128)}, f32[8,1024]{1,0:T(8,128)}, u32[]{:S(2)}, u32[]{:S(2)}) collective-permute-start(f32[8,1024]{1,0:T(8,128)} %collective-permute-done.3.refs_0_), channel_id=1, source_target_pairs={{0,1},{1,0},{2,3},{3,2},{4,5},{5,4},{6,7},{7,6}} | collective-permute-start | bytes 98312 | tf_op jit(solution)/shard_map/ppermute | solution.py:361
  131.4 74.1 %copy-start.2 = (f32[8,1024]{1,0:T(8,128)}, f32[8,1024]{1,0:T(8,128)S(1)}, u32[]{:S(2)}) copy-start(f32[8,1024]{1,0:T(8,128)S(1)} %collective-permute-done.15.refs_0_) | copy-start | bytes 98308
  131.4 74.1 %collective-permute-start.18 = (bf16[1024,768]{1,0:T(8,128)(2,1)}, bf16[1024,768]{1,0:T(8,128)(2,1)}, u32[]{:S(2)}, u32[]{:S(2)}) collective-permute-start(bf16[1024,768]{1,0:T(8,128)(2,1)} %collective-permute-done.16.refs_2_), channel_id=1, source_target_pairs={{0,1},{1,0},{2,3},{3,2},{4,5},{5,4},{6,7},{7,6}} | collective-permute-start | bytes 4718600 | tf_op jit(solution)/shard_map/ppermute | solution.py:361
  131.5 74.1 %collective-permute-start.17 = (f32[8,1024]{1,0:T(8,128)S(1)}, f32[8,1024]{1,0:T(8,128)}, u32[]{:S(2)}, u32[]{:S(2)}) collective-permute-start(f32[8,1024]{1,0:T(8,128)S(1)} %collective-permute-done.15.refs_0_), channel_id=1, source_target_pairs={{0,1},{1,0},{2,3},{3,2},{4,5},{5,4},{6,7},{7,6}} | collective-permute-start | bytes 98312 | tf_op jit(solution)/shard_map/ppermute | solution.py:361
  282.2 8.8 %collective-permute-start.19 = (bf16[1024,768]{1,0:T(8,128)(2,1)}, bf16[1024,768]{1,0:T(8,128)(2,1)S(1)}, u32[]{:S(2)}, u32[]{:S(2)}) collective-permute-start(bf16[1024,768]{1,0:T(8,128)(2,1)} %get-tuple-element.36), channel_id=1, source_target_pairs={{0,1},{1,0},{2,3},{3,2},{4,5},{5,4},{6,7},{7,6}} | collective-permute-start | bytes 4718600 | tf_op jit(solution)/shard_map/ppermute | solution.py:361
  282.3 12.1 %collective-permute-start.6 = (bf16[1024,768]{1,0:T(8,128)(2,1)}, bf16[1024,768]{1,0:T(8,128)(2,1)}, u32[]{:S(2)}, u32[]{:S(2)}) collective-permute-start(bf16[1024,768]{1,0:T(8,128)(2,1)} %get-tuple-element.24), channel_id=1, source_target_pairs={{0,1},{1,0},{2,3},{3,2},{4,5},{5,4},{6,7},{7,6}} | collective-permute-start | bytes 4718600 | tf_op jit(solution)/shard_map/ppermute | solution.py:361
  282.8 41.8 %collective-permute-start.13 = (bf16[1024,768]{1,0:T(8,128)(2,1)}, bf16[1024,768]{1,0:T(8,128)(2,1)}, u32[]{:S(2)}, u32[]{:S(2)}) collective-permute-start(bf16[1024,768]{1,0:T(8,128)(2,1)} %get-tuple-element.31.refs_7_), channel_id=1, source_target_pairs={{0,4},{1,5},{2,6},{3,7},{4,0},{5,1},{6,2},{7,3}} | collective-permute-start | bytes 4718600 | tf_op jit(solution)/shard_map/ppermute | solution.py:361
  289.0 68.6 %collective-permute-start.14 = (bf16[1024,768]{1,0:T(8,128)(2,1)}, bf16[1024,768]{1,0:T(8,128)(2,1)}, u32[]{:S(2)}, u32[]{:S(2)}) collective-permute-start(bf16[1024,768]{1,0:T(8,128)(2,1)} %get-tuple-element.32), channel_id=1, source_target_pairs={{0,5},{1,4},{2,7},{3,6},{4,1},{5,0},{6,3},{7,2}} | collective-permute-start | bytes 4718600 | tf_op jit(solution)/shard_map/ppermute | solution.py:361
  289.0 68.6 %collective-permute-start.10 = (bf16[1024,768]{1,0:T(8,128)(2,1)}, bf16[1024,768]{1,0:T(8,128)(2,1)}, u32[]{:S(2)}, u32[]{:S(2)}) collective-permute-start(bf16[1024,768]{1,0:T(8,128)(2,1)} %get-tuple-element.28), channel_id=1, source_target_pairs={{0,3},{1,2},{2,1},{3,0},{4,7},{5,6},{6,5},{7,4}} | collective-permute-start | bytes 4718600 | tf_op jit(solution)/shard_map/ppermute | solution.py:361
  291.1 69.0 %collective-permute-start.9 = (bf16[1024,768]{1,0:T(8,128)(2,1)}, bf16[1024,768]{1,0:T(8,128)(2,1)}, u32[]{:S(2)}, u32[]{:S(2)}) collective-permute-start(bf16[1024,768]{1,0:T(8,128)(2,1)} %get-tuple-element.27.refs_7_), channel_id=1, source_target_pairs={{0,2},{1,3},{2,0},{3,1},{4,6},{5,7},{6,4},{7,5}} | collective-permute-start | bytes 4718600 | tf_op jit(solution)/shard_map/ppermute | solution.py:361
  404.5 3.6 collective-permute-start.20
  404.6 38.1 %collective-permute-start.21 = (bf16[1024,768]{1,0:T(8,128)(2,1)}, bf16[1024,768]{1,0:T(8,128)(2,1)S(1)}, u32[]{:S(2)}, u32[]{:S(2)}) collective-permute-start(bf16[1024,768]{1,0:T(8,128)(2,1)} %add_convert_fusion.1.refs_13_), channel_id=1, source_target_pairs={{0,6},{1,7},{2,4},{3,5},{4,2},{5,3},{6,0},{7,1}} | collective-permute-start | bytes 4718600 | tf_op jit(solution)/shard_map/ppermute | solution.py:361
